TPU v7x, 512 devices: a 8x2x16 block of a 8x8x16 slice. The times are simulated.
512 devices in a mesh: group: 2 (over y), ha: 16 (over x, core), wa: 16 (over z).
Axes of the slice: x: 8, y: 2, z: 16, core: 2. Of those that a mesh axis runs over, the one named last changes fastest.
The devices are a block of a 8x8x16 slice.
Arguments:
- queries: bfloat16 [4, 128, 128, 1536], P('group', 'ha', 'wa'), parts along dimension 0, may hold values from -6 to 6
- keys: bfloat16 [4, 128, 128, 1536], P('group', 'ha', 'wa'), parts along dimension 0, may hold values from -6 to 6
- values: bfloat16 [4, 128, 128, 1536], P('group', 'ha', 'wa'), parts along dimension 0, may hold values from -6 to 6
- out_grad: bfloat16 [4, 128, 128, 1536], P('group', 'ha', 'wa'), parts along dimension 0, may hold values from -96 to 96
- log_norm: float32 [12, 4, 128, 128], P(None, 'group', 'ha', 'wa'), parts along dimension 1, may hold values from 6.5 to 7.5
- delta_rows: float32 [12, 4, 128, 128], P(None, 'group', 'ha', 'wa'), parts along dimension 1, may hold values from -360 to 360
- text_keys: bfloat16 [64, 1536], P('group'), parts along dimension 0, may hold values from -6 to 6
- text_values: bfloat16 [64, 1536], P('group'), parts along dimension 0, may hold values from -6 to 6
- window_table: int32 [16, 16, 9], replicated, may hold values 0 or 1
Outputs:
- query_grad: bfloat16 [4, 128, 128, 1536], P('group', 'ha', 'wa'), parts along dimension 0
- key_grad: bfloat16 [4, 128, 128, 1536], P('group', 'ha', 'wa'), parts along dimension 0
- value_grad: bfloat16 [4, 128, 128, 1536], P('group', 'ha', 'wa'), parts along dimension 0
- text_key_grad: bfloat16 [64, 1536], P('group'), parts along dimension 0
- text_value_grad: bfloat16 [64, 1536], P('group'), parts along dimension 0
There are 2 independent parts, one for each index of `group`. A program takes and returns all parts, laid end to end along the dimension named above; an argument that names none is the same for every part. Nothing has to cross between parts.
All inputs are finite; a program needn't handle non-finite values.
Results may differ from a plain program's by a relative error of at most 0.001.
The roundings to bfloat16 on the way count: a program that leaves them out, or rounds other values in their place, can miss the bound.
Values may be sent and summed in bfloat16 or wider, within the bound.
A program may use at most 64 MiB of HBM per device.

v0:
```python
import math

import jax
import jax.numpy as jnp
from jax import lax
from jax.sharding import Mesh
from jax.sharding import PartitionSpec as P

HEADS = 12
HDIM = 128
TILE = 8
HALO = 2
HA = ("ha_0", "ha_1")
HA_WA = ("ha_0", "ha_1", "wa")


def passed_along(value, axis, steps):
    count = lax.axis_size(axis)
    pairs = [(source, (source + steps) % count) for source in range(count)]
    return lax.ppermute(value, axis, pairs)


def with_halo(cells, sides, width):
    for axis, dim in sides:
        count = lax.axis_size(axis)
        head = lax.slice_in_dim(cells, 0, width, axis=dim)
        tail = lax.slice_in_dim(cells, cells.shape[dim] - width, cells.shape[dim], axis=dim)
        cells = jnp.concatenate(
            [
                lax.ppermute(tail, axis, [(i, (i + 1) % count) for i in range(count)]),
                cells,
                lax.ppermute(head, axis, [((i + 1) % count, i) for i in range(count)]),
            ],
            axis=dim,
        )
    return cells


def one_axis_at_a_time(shard, axes):
    for axis in axes:
        shard = lax.psum(shard, axis)
    return shard


def tile_grads(query_rows, cotangent_rows, norm_rows, delta_part, key_rows, value_rows, cell_mask):
    score_scale = 1.0 / math.sqrt(query_rows.shape[-1])
    scores = (
        jnp.einsum("qhd,khd->hqk", query_rows, key_rows, preferred_element_type=jnp.float32)
        * score_scale
    )
    probs = jnp.exp(scores - norm_rows[:, :, None])
    if cell_mask is not None:
        probs = probs * cell_mask[None, None, :]
    probs_half = probs.astype(jnp.bfloat16)
    value_part = jnp.einsum(
        "hqk,qhd->khd", probs_half, cotangent_rows, preferred_element_type=jnp.float32
    )
    prob_grad = jnp.einsum(
        "qhd,khd->hqk", cotangent_rows, value_rows, preferred_element_type=jnp.float32
    )
    score_grad = (probs * (prob_grad - delta_part[:, :, None])).astype(jnp.bfloat16)
    query_part = (
        jnp.einsum("hqk,khd->qhd", score_grad, key_rows, preferred_element_type=jnp.float32)
        * score_scale
    )
    key_part = (
        jnp.einsum("hqk,qhd->khd", score_grad, query_rows, preferred_element_type=jnp.float32)
        * score_scale
    )
    return (query_part, key_part, value_part)


def send_cols(strip, offset):
    return passed_along(strip, "wa", offset)


def send_rows(strip, offset):
    return passed_along(strip, HA, offset)


def fold_band(buffer, along, mover):
    lower = lax.slice_in_dim(buffer, 0, HALO, axis=along)
    middle = lax.slice_in_dim(buffer, HALO, HALO + TILE, axis=along)
    upper = lax.slice_in_dim(buffer, HALO + TILE, TILE + 2 * HALO, axis=along)
    from_before = mover(upper, 1)
    from_after = mover(lower, -1)
    widths_low = [(0, 0)] * buffer.ndim
    widths_high = [(0, 0)] * buffer.ndim
    widths_low[along] = (0, TILE - HALO)
    widths_high[along] = (TILE - HALO, 0)
    return middle + jnp.pad(from_before, widths_low) + jnp.pad(from_after, widths_high)


def local(
    queries, keys, values, out_grad, log_norm, delta_rows, text_keys, text_values, window_table
):
    frames, tile_side, _, width = queries.shape
    window_side = TILE + 2 * HALO
    stacked = jnp.stack((keys, values))
    window = with_halo(stacked, ((HA, 2), ("wa", 3)), HALO)
    row_tile = lax.axis_index(HA)
    col_tile = lax.axis_index("wa")
    anchor = jnp.zeros((), jnp.int32)
    pattern = (
        lax.dynamic_slice(window_table, (row_tile, col_tile, anchor), (1, 1, 9))
        .reshape(3, 3)
        .astype(jnp.float32)
    )
    position = jnp.arange(window_side, dtype=jnp.int32)
    block_of = (position >= HALO).astype(jnp.int32) + (position >= HALO + TILE).astype(jnp.int32)
    one_hot = (block_of[:, None] == jnp.arange(3, dtype=jnp.int32)[None, :]).astype(jnp.float32)
    cell_grid = jnp.dot(
        jnp.dot(one_hot, pattern, precision=lax.Precision.HIGHEST),
        one_hot.T,
        precision=lax.Precision.HIGHEST,
    )
    cell_mask = jnp.broadcast_to(cell_grid[None], (frames, window_side, window_side)).reshape(-1)
    query_rows = queries.reshape(-1, HEADS, HDIM)
    cotangent_rows = out_grad.reshape(-1, HEADS, HDIM)
    norm_rows = log_norm.reshape(HEADS, -1)
    delta_part = delta_rows.reshape(HEADS, -1)
    key_rows = window[0].reshape(-1, HEADS, HDIM)
    value_rows = window[1].reshape(-1, HEADS, HDIM)
    video_query, video_key, video_value = tile_grads(
        query_rows, cotangent_rows, norm_rows, delta_part, key_rows, value_rows, cell_mask
    )
    text_query, text_key, text_value = tile_grads(
        query_rows,
        cotangent_rows,
        norm_rows,
        delta_part,
        text_keys.reshape(-1, HEADS, HDIM),
        text_values.reshape(-1, HEADS, HDIM),
        None,
    )
    query_grad = (
        (video_query + text_query).astype(jnp.bfloat16).reshape(frames, tile_side, tile_side, width)
    )
    text_total = one_axis_at_a_time(jnp.stack((text_key, text_value)), HA_WA)
    buffer = jnp.stack((video_key, video_value)).reshape(2, frames, window_side, window_side, width)
    buffer = fold_band(buffer, 3, send_cols)
    buffer = fold_band(buffer, 2, send_rows)
    text_key_grad = text_total[0].reshape(-1, width).astype(jnp.bfloat16)
    text_value_grad = text_total[1].reshape(-1, width).astype(jnp.bfloat16)
    return (
        query_grad,
        buffer[0].astype(jnp.bfloat16),
        buffer[1].astype(jnp.bfloat16),
        text_key_grad,
        text_value_grad,
    )


def solution(mesh):
    split = Mesh(
        mesh.devices.reshape(mesh.shape["group"], 8, 2, mesh.shape["wa"]),
        ("group", "ha_0", "ha_1", "wa"),
    )
    return jax.shard_map(
        local,
        mesh=split,
        in_specs=(
            P("group", HA, "wa", None),
            P("group", HA, "wa", None),
            P("group", HA, "wa", None),
            P("group", HA, "wa", None),
            P(None, "group", HA, "wa"),
            P(None, "group", HA, "wa"),
            P("group", None),
            P("group", None),
            P(),
        ),
        out_specs=(
            P("group", HA, "wa", None),
            P("group", HA, "wa", None),
            P("group", HA, "wa", None),
            P("group", None),
            P("group", None),
        ),
        check_vma=False,
    )
```

profile of v0, /device:TPU:65, one launch (start us, length us, event | category | flops | bytes accessed | tf_op | source)
XLA Modules:
  0.0 264.9 jit_solution(15022201213251635187)
XLA Ops:
  7.2 0.0 copy-start
  7.2 0.1 all-reduce.8.cloned.1.call-start
  7.3 1.1 pad_maximum_fusion.7
  8.4 2.7 %collective-permute-start = (bf16[2,2,2,8,1536]{4,3,2,1,0:T(8,128)(2,1)S(1)}, bf16[2,2,2,8,1536]{4,3,2,1,0:T(8,128)(2,1)S(1)}, u32[]{:S(2)}, u32[]{:S(2)}) collective-permute-start(bf16[2,2,2,8,1536]{4,3,2,1,0:T(8,128)(2,1)S(1)} %get-tuple-element.20), channel_id=1, source_target_pairs={{0,16},{16,32},{32,48},{48,64},{64,80},{80,96},{96,112},{112,128},... | collective-permute-start | bytes 589832 | tf_op jit(solution)/shard_map/ppermute | solution.py:30
  11.1 38.8 %collective-permute-start.1 = (bf16[2,2,2,8,1536]{4,3,2,1,0:T(8,128)(2,1)S(1)}, bf16[2,2,2,8,1536]{4,3,2,1,0:T(8,128)(2,1)S(1)}, u32[]{:S(2)}, u32[]{:S(2)}) collective-permute-start(bf16[2,2,2,8,1536]{4,3,2,1,0:T(8,128)(2,1)S(1)} %get-tuple-element.21), channel_id=1, source_target_pairs={{16,0},{32,16},{48,32},{64,48},{80,64},{96,80},{112,96},{128,112},... | collective-permute-start | bytes 589832 | tf_op jit(solution)/shard_map/ppermute | solution.py:32
  50.0 0.9 copy.34
  50.9 0.9 copy.37
  51.8 1.3 reshape.49
  53.1 0.3 reshape.50
  53.4 0.0 copy-start.4
  53.4 0.0 copy-start.5
  53.4 0.3 fusion.10
  53.8 0.2 convolution_bitcast_fusion.1
  54.0 0.3 fusion.11
  54.3 0.2 fusion.7
  54.5 0.8 pad_maximum_fusion.1
  55.3 0.1 all-reduce.8.cloned.1.call-update
  55.4 0.1 all-reduce.10.cloned.1.call-start
  55.5 1.0 convert_reduce_fusion
  56.4 0.1 convert_element_type.67
  56.5 0.0 collective-permute-done
  56.5 0.0 collective-permute-done.1
  56.6 1.1 pad_maximum_fusion.5
  57.7 1.9 collective-permute-start.2
  59.6 4.9 %collective-permute-start.3 = (bf16[2,2,12,2,1536]{4,3,2,1,0:T(2,128)(2,1)S(1)}, bf16[2,2,12,2,1536]{4,3,2,1,0:T(2,128)(2,1)S(1)}, u32[]{:S(2)}, u32[]{:S(2)}) collective-permute-start(bf16[2,2,12,2,1536]{4,3,2,1,0:T(2,128)(2,1)S(1)} %get-tuple-element.17), channel_id=1, source_target_pairs={{1,0},{2,1},{3,2},{4,3},{5,4},{6,5},{7,6},{8,7},{9,8},{10,9},{11,1... | collective-permute-start | bytes 884744 | tf_op jit(solution)/shard_map/ppermute | solution.py:32
  64.5 0.2 fusion.32
  64.7 0.2 fusion.31
  64.9 0.1 mul.66
  65.0 67.7 %all-reduce.8.cloned.1.call-done = f32[2,32,12,128]{3,1,2,0:T(8,128)} async-done(((f32[2,32,12,128]{3,1,2,0:T(8,128)}), f32[2,32,12,128]{3,1,2,0:T(8,128)}) %all-reduce.8.cloned.1.call-update) | async-done | bytes 393232 | tf_op jit(solution)/shard_map/psum | solution.py:41
  132.8 0.1 all-reduce.10.cloned.1.call-update
  132.9 1.5 pad_maximum_fusion
  134.4 0.2 fusion.38
  134.5 1.7 reshape_squeeze.9
  136.2 0.8 reshape_squeeze.8
  137.0 0.6 exponential_multiply_fusion
  137.6 1.6 convolution_bitcast_fusion
  139.2 0.5 multiply_convert_fusion
  139.7 0.0 copy-start.7
  139.7 0.6 fusion.5
  140.3 0.4 multiply_bitcast_fusion
  140.7 0.3 fusion.6
  141.0 0.4 copy.48
  141.5 1.0 reshape.53
  142.5 2.5 copy.50
  145.0 2.4 stack.30
  147.4 4.0 %copy.52 = f32[288,12,128]{2,1,0:T(8,128)} copy(f32[288,12,128]{2,0,1:T(8,128)} %convolution_bitcast_fusion) | data formatting | bytes 3538944 | tf_op jit(solution)/shard_map/hqk,qhd->khd/transpose | solution.py:55
  151.3 3.2 %stack.31 = f32[1,2,12,12,1536]{4,3,2,1,0:T(8,128)} reshape(f32[288,12,128]{2,1,0:T(8,128)} %copy.52) | data formatting | bytes 3538944 | tf_op jit(solution)/shard_map/stack | solution.py:140
  154.5 0.2 constant_dynamic-update-slice_fusion.1
  154.8 1.4 copy-done.1
  156.2 0.2 constant_dynamic-update-slice_fusion
  156.4 2.1 copy-done.2
  158.5 0.5 fusion.36
  159.0 3.3 %collective-permute-start.4 = (f32[2,2,12,2,1536]{4,3,2,1,0:T(2,128)S(1)}, f32[2,2,12,2,1536]{4,3,2,1,0:T(2,128)S(1)}, u32[]{:S(2)}, u32[]{:S(2)}) collective-permute-start(f32[2,2,12,2,1536]{4,3,2,1,0:T(2,128)S(1)} %get-tuple-element.10), channel_id=1, source_target_pairs={{0,1},{1,2},{2,3},{3,4},{4,5},{5,6},{6,7},{7,8},{8,9},{9,10},{10,1... | collective-permute-start | bytes 1769480 | tf_op jit(solution)/shard_map/ppermute | solution.py:20
  162.3 5.5 %collective-permute-start.5 = (f32[2,2,12,2,1536]{4,3,2,1,0:T(2,128)S(1)}, f32[2,2,12,2,1536]{4,3,2,1,0:T(2,128)S(1)}, u32[]{:S(2)}, u32[]{:S(2)}) collective-permute-start(f32[2,2,12,2,1536]{4,3,2,1,0:T(2,128)S(1)} %get-tuple-element.11), channel_id=1, source_target_pairs={{0,15},{1,0},{2,1},{3,2},{4,3},{5,4},{6,5},{7,6},{8,7},{9,8},{10,9... | collective-permute-start | bytes 1769480 | tf_op jit(solution)/shard_map/ppermute | solution.py:20
  167.8 17.0 %all-reduce.10.cloned.1.call-done = f32[2,32,12,128]{3,1,2,0:T(8,128)} async-done(((f32[2,32,12,128]{3,1,2,0:T(8,128)}), f32[2,32,12,128]{3,1,2,0:T(8,128)}) %all-reduce.10.cloned.1.call-update) | async-done | bytes 393232 | tf_op jit(solution)/shard_map/psum | solution.py:41
  184.8 46.7 %all-reduce.11 = bf16[2,32,12,128]{3,1,2,0:T(8,128)(2,1)S(1)} all-reduce(f32[2,32,12,128]{3,1,2,0:T(8,128)} %all-reduce.10.cloned.1.call-done), channel_id=1, replica_groups=mesh['group'=2,'ha_0'=8,'ha_1'=2,'wa'=16] {'wa'}, use_global_device_ids=true, to_apply=%region_2.0 | all-reduce | flops 98304 | bytes 589824 | tf_op jit(solution)/shard_map/psum | solution.py:41
  231.7 3.0 %fusion = f32[2,2,12,8,1536]{4,3,2,1,0:T(8,128)S(1)} fusion(f32[2,2,12,12,1536]{4,3,2,1,0:T(8,128)} %copy-done.2, f32[2,2,12,2,1536]{4,3,2,1,0:T(2,128)S(1)} %collective-permute-done.5, f32[2,2,12,2,1536]{4,3,2,1,0:T(2,128)S(1)} %collective-permute-done.4), kind=kLoop, calls=%fused_computation.1 | loop fusion | flops 1179648 | bytes 5898240 | tf_op jit(solution)/shard_map/add | solution.py:91
  234.7 0.1 fusion.37
  234.8 15.0 %collective-permute-start.6 = (f32[2,2,2,8,1536]{4,3,2,1,0:T(8,128)S(1)}, f32[2,2,2,8,1536]{4,3,2,1,0:T(8,128)S(1)}, u32[]{:S(2)}, u32[]{:S(2)}) collective-permute-start(f32[2,2,2,8,1536]{4,3,2,1,0:T(8,128)S(1)} %get-tuple-element.12), channel_id=1, source_target_pairs={{0,16},{16,32},{32,48},{48,64},{64,80},{80,96},{96,112},{112,128},... | collective-permute-start | bytes 1179656 | tf_op jit(solution)/shard_map/ppermute | solution.py:20
  249.7 0.7 copy_bitcast_fusion
  250.4 4.0 %collective-permute-done.6 = f32[2,2,2,8,1536]{4,3,2,1,0:T(8,128)S(1)} collective-permute-done((f32[2,2,2,8,1536]{4,3,2,1,0:T(8,128)S(1)}, f32[2,2,2,8,1536]{4,3,2,1,0:T(8,128)S(1)}, u32[]{:S(2)}, u32[]{:S(2)}) %collective-permute-start.6) | collective-permute-done | bytes 393248 | tf_op jit(solution)/shard_map/ppermute | solution.py:20
  254.4 2.5 collective-permute-done.7
  256.9 0.2 fusion.2
  257.1 0.9 slice_bitcast_fusion
  (24 shorter events, 0.2 us)
Async XLA Ops:
  7.2 46.2 %copy-start = (bf16[32,1536]{1,0:T(8,128)(2,1)S(1)}, bf16[32,1536]{1,0:T(8,128)(2,1)}, u32[]{:S(2)}) copy-start(bf16[32,1536]{1,0:T(8,128)(2,1)} %param.15) | copy-start | bytes 294916
  7.2 45.9 %copy-start.8 = (bf16[2,8,8,1536]{3,2,1,0:T(8,128)(2,1)S(1)}, bf16[2,8,8,1536]{3,2,1,0:T(8,128)(2,1)}, u32[]{:S(2)}) copy-start(bf16[2,8,8,1536]{3,2,1,0:T(8,128)(2,1)} %param.12) | copy-start | bytes 1179652
  7.2 125.6 %all-reduce.8.cloned.1.call-start = ((), (), s32[]{:S(2)}) async-start(), calls=%async_computation | async-start | bytes 786432 | tf_op jit(solution)/shard_map/psum | solution.py:41
  7.3 46.7 %copy-start.9 = (bf16[32,1536]{1,0:T(8,128)(2,1)S(1)}, bf16[32,1536]{1,0:T(8,128)(2,1)}, u32[]{:S(2)}) copy-start(bf16[32,1536]{1,0:T(8,128)(2,1)} %param.16) | copy-start | bytes 294916
  8.4 48.1 %collective-permute-start = (bf16[2,2,2,8,1536]{4,3,2,1,0:T(8,128)(2,1)S(1)}, bf16[2,2,2,8,1536]{4,3,2,1,0:T(8,128)(2,1)S(1)}, u32[]{:S(2)}, u32[]{:S(2)}) collective-permute-start(bf16[2,2,2,8,1536]{4,3,2,1,0:T(8,128)(2,1)S(1)} %get-tuple-element.20), channel_id=1, source_target_pairs={{0,16},{16,32},{32,48},{48,64},{64,80},{80,96},{96,112},{112,128},... | collective-permute-start | bytes 589832 | tf_op jit(solution)/shard_map/ppermute | solution.py:30
  11.1 45.4 %collective-permute-start.1 = (bf16[2,2,2,8,1536]{4,3,2,1,0:T(8,128)(2,1)S(1)}, bf16[2,2,2,8,1536]{4,3,2,1,0:T(8,128)(2,1)S(1)}, u32[]{:S(2)}, u32[]{:S(2)}) collective-permute-start(bf16[2,2,2,8,1536]{4,3,2,1,0:T(8,128)(2,1)S(1)} %get-tuple-element.21), channel_id=1, source_target_pairs={{16,0},{32,16},{48,32},{64,48},{80,64},{96,80},{112,96},{128,112},... | collective-permute-start | bytes 589832 | tf_op jit(solution)/shard_map/ppermute | solution.py:32
  53.4 3.2 %copy-start.4 = (bf16[2,8,8,1536]{3,2,1,0:T(8,128)(2,1)S(1)}, bf16[2,8,8,1536]{3,2,1,0:T(8,128)(2,1)}, u32[]{:S(2)}) copy-start(bf16[2,8,8,1536]{3,2,1,0:T(8,128)(2,1)} %param.11) | copy-start | bytes 1179652
  53.4 3.2 %copy-start.5 = (bf16[2,8,8,1536]{3,2,1,0:T(8,128)(2,1)S(1)}, bf16[2,8,8,1536]{3,2,1,0:T(8,128)(2,1)}, u32[]{:S(2)}) copy-start(bf16[2,8,8,1536]{3,2,1,0:T(8,128)(2,1)} %param.10) | copy-start | bytes 1179652
  54.3 78.5 %copy-start.6 = (bf16[12,128,32]{1,2,0:T(8,128)(2,1)}, bf16[12,128,32]{1,2,0:T(8,128)(2,1)S(1)}, u32[]{:S(2)}) copy-start(bf16[12,128,32]{1,2,0:T(8,128)(2,1)S(1)} %fusion.11) | copy-start | bytes 294916
  55.4 129.4 %all-reduce.10.cloned.1.call-start = ((), (), s32[]{:S(2)}) async-start(), calls=%async_computation.1 | async-start | bytes 786432 | tf_op jit(solution)/shard_map/psum | solution.py:41
  57.7 75.1 %collective-permute-start.2 = (bf16[2,2,12,2,1536]{4,3,2,1,0:T(2,128)(2,1)}, bf16[2,2,12,2,1536]{4,3,2,1,0:T(2,128)(2,1)S(1)}, u32[]{:S(2)}, u32[]{:S(2)}) collective-permute-start(bf16[2,2,12,2,1536]{4,3,2,1,0:T(2,128)(2,1)} %get-tuple-element.16), channel_id=1, source_target_pairs={{0,1},{1,2},{2,3},{3,4},{4,5},{5,6},{6,7},{7,8},{8,9},{9,10},{10,1... | collective-permute-start | bytes 884744 | tf_op jit(solution)/shard_map/ppermute | solution.py:30
  59.6 73.2 %collective-permute-start.3 = (bf16[2,2,12,2,1536]{4,3,2,1,0:T(2,128)(2,1)S(1)}, bf16[2,2,12,2,1536]{4,3,2,1,0:T(2,128)(2,1)S(1)}, u32[]{:S(2)}, u32[]{:S(2)}) collective-permute-start(bf16[2,2,12,2,1536]{4,3,2,1,0:T(2,128)(2,1)S(1)} %get-tuple-element.17), channel_id=1, source_target_pairs={{1,0},{2,1},{3,2},{4,3},{5,4},{6,5},{7,6},{8,7},{9,8},{10,9},{11,1... | collective-permute-start | bytes 884744 | tf_op jit(solution)/shard_map/ppermute | solution.py:32
  137.6 1.6 copy-start.3
  139.7 1.0 copy-start.7
  154.5 1.7 copy-start.1
  156.4 2.1 copy-start.2
  159.0 72.6 %collective-permute-start.4 = (f32[2,2,12,2,1536]{4,3,2,1,0:T(2,128)S(1)}, f32[2,2,12,2,1536]{4,3,2,1,0:T(2,128)S(1)}, u32[]{:S(2)}, u32[]{:S(2)}) collective-permute-start(f32[2,2,12,2,1536]{4,3,2,1,0:T(2,128)S(1)} %get-tuple-element.10), channel_id=1, source_target_pairs={{0,1},{1,2},{2,3},{3,4},{4,5},{5,6},{6,7},{7,8},{8,9},{9,10},{10,1... | collective-permute-start | bytes 1769480 | tf_op jit(solution)/shard_map/ppermute | solution.py:20
  162.3 69.4 %collective-permute-start.5 = (f32[2,2,12,2,1536]{4,3,2,1,0:T(2,128)S(1)}, f32[2,2,12,2,1536]{4,3,2,1,0:T(2,128)S(1)}, u32[]{:S(2)}, u32[]{:S(2)}) collective-permute-start(f32[2,2,12,2,1536]{4,3,2,1,0:T(2,128)S(1)} %get-tuple-element.11), channel_id=1, source_target_pairs={{0,15},{1,0},{2,1},{3,2},{4,3},{5,4},{6,5},{7,6},{8,7},{9,8},{10,9... | collective-permute-start | bytes 1769480 | tf_op jit(solution)/shard_map/ppermute | solution.py:20
  234.8 19.7 %collective-permute-start.6 = (f32[2,2,2,8,1536]{4,3,2,1,0:T(8,128)S(1)}, f32[2,2,2,8,1536]{4,3,2,1,0:T(8,128)S(1)}, u32[]{:S(2)}, u32[]{:S(2)}) collective-permute-start(f32[2,2,2,8,1536]{4,3,2,1,0:T(8,128)S(1)} %get-tuple-element.12), channel_id=1, source_target_pairs={{0,16},{16,32},{32,48},{48,64},{64,80},{80,96},{96,112},{112,128},... | collective-permute-start | bytes 1179656 | tf_op jit(solution)/shard_map/ppermute | solution.py:20
  249.7 7.2 %collective-permute-start.7 = (f32[2,2,2,8,1536]{4,3,2,1,0:T(8,128)S(1)}, f32[2,2,2,8,1536]{4,3,2,1,0:T(8,128)S(1)}, u32[]{:S(2)}, u32[]{:S(2)}) collective-permute-start(f32[2,2,2,8,1536]{4,3,2,1,0:T(8,128)S(1)} %get-tuple-element.13), channel_id=1, source_target_pairs={{0,240},{16,0},{32,16},{48,32},{64,48},{80,64},{96,80},{112,96},{1... | collective-permute-start | bytes 1179656 | tf_op jit(solution)/shard_map/ppermute | solution.py:20
Sparse Core Ops, SparseCore 0:
  55.5 77.2 all-reduce.7
  135.7 49.0 all-reduce.9
where the time goes:
time: 267 us; the launch traced here: 265 us
  waiting for transfers between devices  91.4 us (34%)
  starting transfers between devices  72.2 us (27%)
  blocking collectives  46.7 us (17%)
  local copies, waits for them, and re-layouts  26 us (10%)
  between operations  14.4 us (5%)
  other arithmetic  8.7 us (3%)
  matrix products  5.44 us (2%)
    psum x2, waiting for transfers between devices, one_axis_at_a_time(): shard = lax.psum(shard, axis)  84.8 us
    psum x1, blocking collectives, one_axis_at_a_time(): shard = lax.psum(shard, axis)  46.7 us
    ppermute x2, starting transfers between devices, with_halo(): lax.ppermute(head, axis, [((i + 1) % count, i) for i in range(count)])  43.7 us
    ppermute x4, starting transfers between devices, passed_along(): return lax.ppermute(value, axis, pairs)  23.7 us
    ppermute x4, waiting for transfers between devices, passed_along(): return lax.ppermute(value, axis, pairs)  6.49 us
    another operation x3, local copies, waits for them, and re-layouts, local(): jnp.stack((video_key, video_value))  5.77 us
  transfers between devices with their start and end apart: 10, of which 4 were waited for; matrix products, arithmetic and copies ran while one was open for 12% of the time, Pallas kernels for 0%

commit v1 on v0

v1 whole, which is shorter than its diff:
```python
import functools
import math

import jax
import jax.numpy as jnp
import numpy as np
from jax import lax
from jax.experimental import pallas as pl
from jax.experimental.pallas import tpu as pltpu
from jax.sharding import PartitionSpec as P

HEADS = 12
HDIM = 128
TILE = 8
HALO = 2
FRAMES = 2
WIDTH = HEADS * HDIM
CELLS = FRAMES * TILE * TILE
TEXT = 32
CHUNKS = 3
PER_CHUNK = HEADS // CHUNKS
LANES = PER_CHUNK * HDIM
TILES = HEADS * TEXT // 8
SCALE = 1.0 / math.sqrt(HDIM)

TOP, RIGHT, BOTTOM, LEFT, LAST = 4, 7, 10, 13, 16
UP, UP_LEFT, UP_RIGHT, DOWN, DOWN_LEFT, DOWN_RIGHT, WEST, EAST, BORROWED = 0, 4, 5, 6, 10, 11, 12, 16, 20

F32 = jnp.float32
BF16 = jnp.bfloat16
NT = (((1,), (1,)), ((), ()))
NN = (((1,), (0,)), ((), ()))
TN = (((0,), (0,)), ((), ()))


def dot(left, right, dims, precision=None):
    return lax.dot_general(left, right, dims, precision=precision, preferred_element_type=F32)


def region_rows():
    low, mid, high = range(0, HALO), range(HALO, TILE - HALO), range(TILE - HALO, TILE)
    regions = (
        (mid, mid), (low, low), (low, mid), (low, high), (mid, high),
        (high, high), (high, mid), (high, low), (mid, low), (low, low),
    )
    return [
        (frame * TILE + row) * TILE + col
        for rows, cols in regions
        for frame in range(FRAMES)
        for row in rows
        for col in cols
    ]


def tile_grads(key, value, query, cotangent, norm, delta, mask):
    scores = dot(key, query, NT) * SCALE
    probs = jnp.exp(scores - norm)
    if mask is not None:
        probs = probs * mask
    prob_grad = dot(value, cotangent, NT)
    score_grad = (probs * (prob_grad - delta)).astype(BF16)
    value_part = dot(probs.astype(BF16), cotangent, NN)
    key_part = dot(score_grad, query, NN)
    query_part = dot(score_grad, key, TN)
    return query_part, key_part, value_part


def kernel(
    n_ha, n_wa,
    q_hbm, k_hbm, v_hbm, o_hbm, norm_hbm, delta_hbm, tk_hbm, tv_hbm, table, order_hbm, back_hbm,
    dq_out, dk_out, dv_out, text_out,
    q, k, v, o, norm4, delta4, tk, tv, order, back,
    norm, delta, mask, packed, own, halo, rim, rows_in, cols_in, acc, dq,
    tpart, tsib, tchip, xin, zpart, zin, zdup, zall, tfin,
    load_sem, halo_send, halo_recv, rows_send, rows_recv, cols_send, cols_recv,
    pair_send, pair_recv, x_send, x_recv, z_send, z_recv, za_send, za_recv, xa_send, xa_recv,
):
    n_x = n_ha // 2
    owned = TILES // n_x
    ha, wa = lax.axis_index("ha"), lax.axis_index("wa")
    x, core = ha // 2, ha % 2
    up, down = (ha + n_ha - 1) % n_ha, (ha + 1) % n_ha
    left, right = (wa + n_wa - 1) % n_wa, (wa + 1) % n_wa
    sibling = 2 * x + 1 - core

    def remote(src, dst, send, recv, **where):
        return pltpu.make_async_remote_copy(
            src_ref=src, dst_ref=dst, send_sem=send, recv_sem=recv,
            device_id=where, device_id_type=pl.DeviceIdType.MESH,
        )

    def wait_bytes(ref, sem):
        pltpu.make_async_copy(ref, ref, sem).wait()

    barrier = pltpu.get_barrier_semaphore()
    greeted = [{"ha": (ha + 2 * step) % n_ha} for step in range(1, n_x)]
    greeted += [{"ha": up}, {"ha": down}]
    greeted += [{"ha": row, "wa": col} for row in (up, down) for col in (left, right)]
    greeted += [{"wa": left}, {"wa": right}]
    for where in greeted:
        pl.semaphore_signal(barrier, inc=1, device_id=where, device_id_type=pl.DeviceIdType.MESH)

    @pl.when(wa == 0)
    def _():
        for col in range(1, n_wa):
            pl.semaphore_signal(barrier, inc=1, device_id={"wa": col}, device_id_type=pl.DeviceIdType.MESH)

    loads = [
        pltpu.make_async_copy(src, dst, load_sem.at[at])
        for at, (src, dst) in enumerate((
            (norm_hbm, norm4), (delta_hbm, delta4), (tk_hbm, tk), (tv_hbm, tv), (q_hbm, q), (o_hbm, o),
            (order_hbm, order), (k_hbm, k), (v_hbm, v), (back_hbm, back),
        ))
    ]
    for load in loads:
        load.start()

    for load, src, dst in ((loads[0], norm4, norm), (loads[1], delta4, delta)):
        load.wait()
        dst[0:HEADS, :] = src[...].T

    for load in loads[2:6]:
        load.wait()
    for head in range(HEADS):
        at = pl.ds(head * HDIM, HDIM)
        query_part, key_part, value_part = tile_grads(
            tk[:, at], tv[:, at], q[:, at], o[:, at], norm[head:head + 1, :], delta[head:head + 1, :], None
        )
        dq[:, at] = query_part
        tpart[0, 4 * head:4 * head + 4] = (key_part * SCALE).reshape(4, 8, HDIM)
        tpart[1, 4 * head:4 * head + 4] = value_part.reshape(4, 8, HDIM)

    for load in loads[6:10]:
        load.wait()
    for at, src in ((0, k), (1, v)):
        for chunk in range(CHUNKS):
            lanes = pl.ds(chunk * LANES, LANES)
            moved = dot(order[...], src[:, lanes], NN)
            packed[at, :, :, lanes] = moved.reshape(LAST + 1, 8, LANES).astype(BF16)
            own[at, :, lanes] = moved[0:CELLS].astype(BF16)

    live = [table[block, ha, wa].astype(F32) for block in range(9)]
    for start, count, block in (
        (UP, 4, 1), (UP_LEFT, 1, 0), (UP_RIGHT, 1, 2), (DOWN, 4, 7), (DOWN_LEFT, 1, 6), (DOWN_RIGHT, 1, 8),
        (WEST, 4, 3), (EAST, 4, 5),
    ):
        mask[8 * start:8 * (start + count), :] = jnp.full((8 * count, CELLS), live[block], F32)

    pl.semaphore_wait(barrier, len(greeted) + jnp.where(wa == 0, 0, 1))

    pair = remote(tpart.at[1 - core], tsib, pair_send.at[0], pair_recv.at[0], ha=sibling)
    pair.start()

    def send_halo(chunk):
        lanes = pl.ds(chunk * LANES, LANES)
        for src, dst, count, where in (
            (LEFT, EAST, 4, {"wa": left}),
            (RIGHT, WEST, 4, {"wa": right}),
            (TOP, DOWN, 4, {"ha": up}),
            (BOTTOM, UP, 4, {"ha": down}),
            (TOP, DOWN_RIGHT, 1, {"ha": up, "wa": left}),
            (RIGHT, DOWN_LEFT, 1, {"ha": up, "wa": right}),
            (LEFT, UP_RIGHT, 1, {"ha": down, "wa": left}),
            (BOTTOM, UP_LEFT, 1, {"ha": down, "wa": right}),
        ):
            remote(
                packed.at[:, src:src + count, :, lanes], halo.at[:, dst:dst + count, :, lanes],
                halo_send.at[chunk], halo_recv.at[chunk], **where,
            ).start()

    send_halo(0)

    pair.wait()
    tchip[...] = (tpart[core] + tsib[...]).reshape(n_x, owned, 8, HDIM)
    for step in range(1, n_x):
        to = (x + step) % n_x
        remote(tchip.at[to], xin.at[step - 1], x_send.at[0], x_recv.at[0], ha=2 * to + core).start()

    for chunk in range(1, CHUNKS):
        send_halo(chunk)

    for head in range(HEADS):
        at = pl.ds(head * HDIM, HDIM)
        query_part, key_part, value_part = tile_grads(
            own[0, :, at], own[1, :, at], q[:, at], o[:, at],
            norm[head:head + 1, :], delta[head:head + 1, :], live[4],
        )
        dq[:, at] += query_part
        acc[0, :, :, at] = key_part.reshape(CELLS // 8, 8, HDIM)
        acc[1, :, :, at] = value_part.reshape(CELLS // 8, 8, HDIM)

    def rim_grads(chunk):
        lanes = pl.ds(chunk * LANES, LANES)
        wait_bytes(halo.at[:, :, :, lanes], halo_recv.at[chunk])
        for head in range(chunk * PER_CHUNK, (chunk + 1) * PER_CHUNK):
            at = pl.ds(head * HDIM, HDIM)
            query_part, key_part, value_part = tile_grads(
                halo[0, :, :, at].reshape(8 * BORROWED, HDIM), halo[1, :, :, at].reshape(8 * BORROWED, HDIM),
                q[:, at], o[:, at], norm[head:head + 1, :], delta[head:head + 1, :], mask[...],
            )
            dq[:, at] += query_part
            rim[0, :, :, at] = key_part.reshape(BORROWED, 8, HDIM)
            rim[1, :, :, at] = value_part.reshape(BORROWED, 8, HDIM)
        for side, start, where in ((0, UP, up), (1, DOWN, down)):
            remote(
                rim.at[:, start:start + 6, :, lanes], rows_in.at[side, :, :, :, lanes],
                rows_send.at[side, chunk], rows_recv.at[side, chunk], ha=where,
            ).start()

    def cols_out(chunk):
        lanes = pl.ds(chunk * LANES, LANES)
        for side in range(2):
            wait_bytes(rows_in.at[side, :, :, :, lanes], rows_recv.at[side, chunk])
        rim[:, WEST, :, lanes] += rows_in[1, :, 4, :, lanes]
        rim[:, WEST + 3, :, lanes] += rows_in[0, :, 4, :, lanes]
        rim[:, EAST, :, lanes] += rows_in[0, :, 5, :, lanes]
        rim[:, EAST + 3, :, lanes] += rows_in[1, :, 5, :, lanes]
        for side, start, where in ((0, WEST, left), (1, EAST, right)):
            remote(
                rim.at[:, start:start + 4, :, lanes], cols_in.at[side, :, :, :, lanes],
                cols_send.at[side, chunk], cols_recv.at[side, chunk], wa=where,
            ).start()

    def finish(chunk):
        lanes = pl.ds(chunk * LANES, LANES)
        acc[:, BOTTOM:BOTTOM + 4, :, lanes] += rows_in[0, :, 0:4, :, lanes]
        acc[:, TOP:TOP + 4, :, lanes] += rows_in[1, :, 0:4, :, lanes]
        for side in range(2):
            wait_bytes(cols_in.at[side, :, :, :, lanes], cols_recv.at[side, chunk])
        acc[:, RIGHT:RIGHT + 4, :, lanes] += cols_in[0, :, :, :, lanes]
        acc[:, LEFT:LEFT + 3, :, lanes] += cols_in[1, :, 0:3, :, lanes]
        acc[:, TOP, :, lanes] += cols_in[1, :, 3, :, lanes]
        for at, out, factor in ((0, dk_out, SCALE), (1, dv_out, 1.0)):
            total = (acc[at, :, :, lanes] * factor).reshape(CELLS, LANES).astype(BF16)
            out[:, lanes] = dot(back[...], total, NN).astype(BF16)

    def gather_x():
        tfin[core, x] = zall[...]
        for step in range(1, n_x):
            to = (x + step) % n_x
            remote(zall, tfin.at[core, x], xa_send.at[0], xa_recv.at[0], ha=2 * to + core).start()

    rim_grads(0)
    rim_grads(1)

    wait_bytes(xin, x_recv.at[0])
    total = tchip[x]
    for step in range(n_x - 1):
        total = total + xin[step]
    zpart[...] = total

    @pl.when(wa != 0)
    def _():
        remote(zpart, zin.at[wa - 1], z_send.at[0], z_recv.at[0], wa=0).start()

    rim_grads(2)
    cols_out(0)
    cols_out(1)

    @pl.when(wa == 0)
    def _():
        wait_bytes(zin, z_recv.at[0])
        final = zpart[...]
        for col in range(n_wa - 1):
            final = final + zin[col]
        final = final.astype(BF16)
        zall[...] = final
        gather_x()
        for col in range(1, n_wa):
            remote(zall, zall, za_send.at[0], za_recv.at[0], wa=col).start()

    cols_out(2)
    dq_out[...] = (dq[...] * SCALE).astype(BF16)
    finish(0)
    finish(1)

    @pl.when(wa != 0)
    def _():
        wait_bytes(zall, za_recv.at[0])
        gather_x()

    finish(2)

    wait_bytes(tfin.at[core, 0:n_x - 1], xa_recv.at[0])
    pair = remote(tfin.at[core], tfin.at[core], pair_send.at[1], pair_recv.at[1], ha=sibling)
    pair.start()
    wait_bytes(tfin.at[1 - core], pair_recv.at[1])
    for at in range(2):
        for tile in range(TILES):
            text_out[at, tile % 4, :, (tile // 4) * HDIM:(tile // 4 + 1) * HDIM] = tfin[at, tile // owned, tile % owned]
    pair.wait_send()
    for chunk in range(CHUNKS):
        lanes = pl.ds(chunk * LANES, LANES)
        wait_bytes(halo.at[:, :, :, lanes], halo_send.at[chunk])
        for side in range(2):
            wait_bytes(rows_in.at[side, :, :, :, lanes], rows_send.at[side, chunk])
            wait_bytes(cols_in.at[side, :, :, :, lanes], cols_send.at[side, chunk])
    wait_bytes(xin, x_send.at[0])
    @pl.when(wa != 0)
    def _():
        wait_bytes(zpart, z_send.at[0])

    @pl.when(wa == 0)
    def _():
        wait_bytes(zdup, za_send.at[0])

    wait_bytes(tfin.at[core, 0:n_x - 1], xa_send.at[0])


def store(dq, dk, dv, text, dq_hbm, dk_hbm, dv_hbm, dtk_hbm, dtv_hbm, sem):
    copies = [
        pltpu.make_async_copy(src, dst, sem.at[at])
        for at, (src, dst) in enumerate((
            (dq, dq_hbm), (dk, dk_hbm), (dv, dv_hbm), (text.at[0], dtk_hbm), (text.at[1], dtv_hbm),
        ))
    ]
    for copy in copies:
        copy.start()
    for copy in copies:
        copy.wait()


def local(n_ha, n_wa, queries, keys, values, out_grad, log_norm, delta_rows, text_keys, text_values, window_table):
    n_x = n_ha // 2
    owned = TILES // n_x
    rows = region_rows()
    order = np.zeros((8 * (LAST + 1), CELLS), np.float32)
    order[np.arange(len(rows)), rows] = 1.0
    back = order[:CELLS].T
    hbm = pl.BlockSpec(memory_space=pl.ANY)
    vmem = pltpu.VMEM
    dma = pltpu.SemaphoreType.DMA
    flat = (CELLS, WIDTH)
    outs = pl.pallas_call(
        functools.partial(kernel, n_ha, n_wa),
        out_shape=[vmem(flat, BF16)] * 3 + [vmem((2, TEXT // 8, 8, WIDTH), BF16)],
        in_specs=[hbm] * 8 + [pl.BlockSpec(memory_space=pltpu.SMEM)] + [hbm] * 2,
        out_specs=[pl.BlockSpec(memory_space=vmem)] * 4,
        scratch_shapes=[
            vmem(flat, BF16), vmem(flat, BF16), vmem(flat, BF16), vmem(flat, BF16),
            vmem((CELLS, HEADS), F32), vmem((CELLS, HEADS), F32),
            vmem((TEXT, WIDTH), BF16), vmem((TEXT, WIDTH), BF16),
            vmem((8 * (LAST + 1), CELLS), BF16), vmem((CELLS, CELLS), BF16),
            vmem((16, CELLS), F32), vmem((16, CELLS), F32), vmem((8 * BORROWED, CELLS), F32),
            vmem((2, LAST + 1, 8, WIDTH), BF16), vmem((2, CELLS, WIDTH), BF16),
            vmem((2, BORROWED, 8, WIDTH), BF16), vmem((2, BORROWED, 8, WIDTH), F32),
            vmem((2, 2, 6, 8, WIDTH), F32), vmem((2, 2, 4, 8, WIDTH), F32),
            vmem((2, CELLS // 8, 8, WIDTH), F32), vmem(flat, F32),
            vmem((2, TILES, 8, HDIM), F32), vmem((TILES, 8, HDIM), F32), vmem((n_x, owned, 8, HDIM), F32),
            vmem((n_x - 1, owned, 8, HDIM), F32), vmem((owned, 8, HDIM), F32), vmem((n_wa - 1, owned, 8, HDIM), F32),
            vmem((n_wa - 1, owned, 8, HDIM), BF16), vmem((owned, 8, HDIM), BF16), vmem((2, n_x, owned, 8, HDIM), BF16),
            dma((10,)), dma((CHUNKS,)), dma((CHUNKS,)),
            dma((2, CHUNKS)), dma((2, CHUNKS)), dma((2, CHUNKS)), dma((2, CHUNKS)),
            dma((2,)), dma((2,)), dma((1,)), dma((1,)), dma((1,)), dma((1,)),
            dma((1,)), dma((1,)), dma((1,)), dma((1,)),
        ],
        compiler_params=pltpu.CompilerParams(collective_id=0, has_side_effects=True, vmem_limit_bytes=56 << 20),
    )(
        queries.reshape(flat), keys.reshape(flat), values.reshape(flat), out_grad.reshape(flat),
        log_norm.transpose(1, 2, 3, 0).reshape(CELLS, HEADS), delta_rows.transpose(1, 2, 3, 0).reshape(CELLS, HEADS),
        text_keys, text_values, window_table.transpose(2, 0, 1),
        jnp.asarray(order, BF16), jnp.asarray(back, BF16),
    )
    outs = pl.pallas_call(
        store,
        out_shape=[jax.ShapeDtypeStruct(flat, BF16)] * 3 + [jax.ShapeDtypeStruct((TEXT // 8, 8, WIDTH), BF16)] * 2,
        in_specs=[pl.BlockSpec(memory_space=vmem)] * 4,
        out_specs=[hbm] * 5,
        scratch_shapes=[dma((5,))],
        compiler_params=pltpu.CompilerParams(has_side_effects=True, vmem_limit_bytes=1 << 20),
    )(*outs)
    cells = queries.shape
    return (
        outs[0].reshape(cells), outs[1].reshape(cells), outs[2].reshape(cells),
        outs[3].reshape(TEXT, WIDTH), outs[4].reshape(TEXT, WIDTH),
    )


def solution(mesh):
    cells = P("group", "ha", "wa", None)
    stats = P(None, "group", "ha", "wa")
    text = P("group", None)
    return jax.shard_map(
        functools.partial(local, mesh.shape["ha"], mesh.shape["wa"]),
        mesh=mesh,
        in_specs=(cells, cells, cells, cells, stats, stats, text, text, P()),
        out_specs=(cells, cells, cells, text, text),
        check_vma=False,
    )
```

time: 267 us -> 78.9 us (0.30)
  the two profiles are of different devices: /device:TPU:65 before, /device:TPU:209 now
where the time goes in v1:
time: 78.9 us; the launch traced here: 78.6 us
  Pallas kernels  78 us (99%)
    pallas_call x1, Pallas kernels, local(): pl.pallas_call(functools.partial(kernel, n_ha, n_wa), out_shape=[vmem(fla...  76.9 us

profile of v1, /device:TPU:209, one launch (start us, length us, event | category | flops | bytes accessed | tf_op | source)
XLA Modules:
  0.0 78.6 jit_solution(55348941790577012)
XLA Ops:
  0.6 76.9 %shard_map.146 = (bf16[128,1536]{1,0:T(8,128)(2,1)S(1)}, bf16[128,1536]{1,0:T(8,128)(2,1)S(1)}, bf16[128,1536]{1,0:T(8,128)(2,1)S(1)}, bf16[2,4,8,1536]{3,2,1,0:T(8,128)(2,1)S(1)}) custom-call(bf16[128,1536]{1,0:T(8,128)(2,1)} %bitcast.16, bf16[128,1536]{1,0:T(8,128)(2,1)} %bitcast.17, bf16[128,1536]{1,0:T(8,128)(2,1)} %bitcast.18, ...), custom_call_target="tpu_custom_call" | custom-call | tf_op jit(solution)/shard_map/pallas_call | solution.py:334
  77.5 1.1 %shard_map.147 = (bf16[128,1536]{1,0:T(8,128)(2,1)}, bf16[128,1536]{1,0:T(8,128)(2,1)}, bf16[128,1536]{1,0:T(8,128)(2,1)}, bf16[4,8,1536]{2,1,0:T(8,128)(2,1)}, bf16[4,8,1536]{2,1,0:T(8,128)(2,1)}) custom-call(bf16[128,1536]{1,0:T(8,128)(2,1)S(1)} %get-tuple-element.14.dq, bf16[128,1536]{1,0:T(8,128)(2,1)S(1)} %get-tuple-element.15.dk, ...), custom_call_target="tpu_custom_call" | custom-call | tf_op jit(solution)/shard_map/pallas_call | solution.py:364

commit v2 on v1

v2 whole, which is shorter than its diff:
```python
import functools
import math

import jax
import jax.numpy as jnp
import numpy as np
from jax import lax
from jax.experimental import pallas as pl
from jax.experimental.pallas import tpu as pltpu
from jax.sharding import PartitionSpec as P

HEADS = 12
HDIM = 128
TILE = 8
HALO = 2
FRAMES = 2
WIDTH = HEADS * HDIM
CELLS = FRAMES * TILE * TILE
TEXT = 32
CHUNKS = 3
PER_CHUNK = HEADS // CHUNKS
LANES = PER_CHUNK * HDIM
TILES = HEADS * TEXT // 8
SCALE = 1.0 / math.sqrt(HDIM)

TOP, RIGHT, BOTTOM, LEFT, LAST = 4, 7, 10, 13, 16
EAST, UP_RIGHT, DOWN_RIGHT, UP, DOWN, WEST, UP_LEFT, DOWN_LEFT, BORROWED = 0, 4, 5, 6, 10, 14, 18, 19, 20
PARTS = ((0, 6), (6, 14), (14, 20))

F32 = jnp.float32
BF16 = jnp.bfloat16
NT = (((1,), (1,)), ((), ()))
NN = (((1,), (0,)), ((), ()))
TN = (((0,), (0,)), ((), ()))


def dot(left, right, dims, precision=None):
    return lax.dot_general(left, right, dims, precision=precision, preferred_element_type=F32)


def region_rows():
    low, mid, high = range(0, HALO), range(HALO, TILE - HALO), range(TILE - HALO, TILE)
    regions = (
        (mid, mid), (low, low), (low, mid), (low, high), (mid, high),
        (high, high), (high, mid), (high, low), (mid, low), (low, low),
    )
    return [
        (frame * TILE + row) * TILE + col
        for rows, cols in regions
        for frame in range(FRAMES)
        for row in rows
        for col in cols
    ]


def score_grads(key, value, query, cotangent, norm, delta, mask):
    probs = jnp.exp(dot(key, query, NT) * SCALE - norm)
    if mask is not None:
        probs = probs * mask
    score_grad = (probs * (dot(value, cotangent, NT) - delta)).astype(BF16)
    return probs.astype(BF16), score_grad


def kernel(
    n_ha, n_wa,
    q_hbm, k_hbm, v_hbm, o_hbm, norm_hbm, delta_hbm, tk_hbm, tv_hbm, table_hbm, order_hbm, back_hbm,
    dq_out, dk_out, dv_out, text_out,
    q, k, v, o, norm12, delta12, tk, tv, order, back, table,
    norm, delta, mask, packed, own, halo, rim, rows_in, corner_in, cols_in, acc, dq, text_grad,
    tpart, tsib, tchip, xin, zpart, zin, zall, tfin,
    load_sem, halo_send, halo_recv, rows_send, rows_recv, corner_send, corner_recv, cols_send, cols_recv,
    pair_send, pair_recv, x_send, x_recv, z_send, z_recv, za_send, za_recv, xa_send, xa_recv, ready,
):
    n_x = n_ha // 2
    owned = TILES // n_x
    ha, wa = lax.axis_index("ha"), lax.axis_index("wa")
    x, core = ha // 2, ha % 2
    up, down = (ha + n_ha - 1) % n_ha, (ha + 1) % n_ha
    left, right = (wa + n_wa - 1) % n_wa, (wa + 1) % n_wa
    sibling = 2 * x + 1 - core

    def remote(src, dst, send, recv, **where):
        return pltpu.make_async_remote_copy(
            src_ref=src, dst_ref=dst, send_sem=send, recv_sem=recv,
            device_id=where, device_id_type=pl.DeviceIdType.MESH,
        )

    def signal(sem, **where):
        pl.semaphore_signal(sem, inc=1, device_id=where, device_id_type=pl.DeviceIdType.MESH)

    def wait_bytes(ref, sem):
        pltpu.make_async_copy(ref, ref, sem).wait()

    def lanes_of(chunk):
        return pl.ds(chunk * LANES, LANES)

    barrier = pltpu.get_barrier_semaphore()
    for col in (left,):
        signal(barrier, wa=col)
        signal(barrier, ha=up, wa=col)
        signal(barrier, ha=down, wa=col)
    signal(barrier, ha=up)
    signal(barrier, ha=down)
    for step in range(1, n_x):
        signal(barrier, ha=(ha + 2 * step) % n_ha)

    loads = [
        pltpu.make_async_copy(src, dst, load_sem.at[at])
        for at, (src, dst) in enumerate((
            (k_hbm, k), (v_hbm, v), (order_hbm, order), (norm_hbm, norm12), (delta_hbm, delta12),
            (tk_hbm, tk), (tv_hbm, tv), (q_hbm, q), (o_hbm, o), (table_hbm, table), (back_hbm, back),
        ))
    ]
    for load in loads:
        load.start()

    @pl.when(wa == 0)
    def _():
        for col in range(1, n_wa):
            signal(barrier, wa=col)

    def send_halo(part, chunk, sends):
        lanes = lanes_of(chunk)
        for src, dst, count, where in sends:
            to_part = [at for at, (low, high) in enumerate(PARTS) if low <= dst < high][0]
            remote(
                packed.at[:, src:src + count, :, lanes], halo.at[:, dst:dst + count, :, lanes],
                halo_send.at[part, chunk], halo_recv.at[to_part, chunk], **where,
            ).start()

    def enter():
        pl.semaphore_wait(barrier, 5 + n_x - 1 + jnp.where(wa == 0, 0, 1))
        signal(ready.at[0], wa=right)
        signal(ready.at[1], ha=up, wa=right)
        signal(ready.at[1], ha=down, wa=right)
        for chunk in range(CHUNKS):
            send_halo(0, chunk, (
                (RIGHT, WEST, 4, {"wa": right}),
                (RIGHT, DOWN_LEFT, 1, {"ha": up, "wa": right}),
                (BOTTOM, UP_LEFT, 1, {"ha": down, "wa": right}),
            ))
            send_halo(1, chunk, ((TOP, DOWN, 4, {"ha": up}), (BOTTOM, UP, 4, {"ha": down})))

    def send_west():
        pl.semaphore_wait(ready.at[0], 1)
        for chunk in range(CHUNKS):
            send_halo(2, chunk, ((LEFT, EAST, 4, {"wa": left}),))
        pl.semaphore_wait(ready.at[1], 2)
        for chunk in range(CHUNKS):
            send_halo(2, chunk, (
                (TOP, DOWN_RIGHT, 1, {"ha": up, "wa": left}),
                (LEFT, UP_RIGHT, 1, {"ha": down, "wa": left}),
            ))

    for load in loads[0:3]:
        load.wait()
    for at, src in ((0, k), (1, v)):
        for chunk in range(CHUNKS):
            moved = dot(order[...], src[:, lanes_of(chunk)], NN)
            packed[at, :, :, lanes_of(chunk)] = moved.reshape(LAST + 1, 8, LANES).astype(BF16)
            own[at, :, lanes_of(chunk)] = moved[0:CELLS].astype(BF16)

    late = (wa == n_wa - 1) | ((wa == 0) & (ha == 0))
    pl.when(late)(enter)

    for load, src, dst in ((loads[3], norm12, norm), (loads[4], delta12, delta)):
        load.wait()
        dst[0:HEADS, :] = src[...].T

    def statistics(head):
        return norm[head:head + 1, :], delta[head:head + 1, :]

    for load in loads[5:9]:
        load.wait()
    for head in range(HEADS):
        at = pl.ds(head * HDIM, HDIM)
        probs, score_grad = score_grads(tk[:, at], tv[:, at], q[:, at], o[:, at], *statistics(head), None)
        text_grad[head] = score_grad
        tpart[0, 4 * head:4 * head + 4] = (dot(score_grad, q[:, at], NN) * SCALE).reshape(4, 8, HDIM)
        tpart[1, 4 * head:4 * head + 4] = dot(probs, o[:, at], NN).reshape(4, 8, HDIM)

    pl.when(jnp.logical_not(late))(enter)

    pair = remote(tpart.at[1 - core], tsib, pair_send.at[0], pair_recv.at[0], ha=sibling)
    pair.start()

    pl.when(wa != 0)(send_west)

    for load in loads[9:11]:
        load.wait()
    live = [table[block, ha, wa].astype(F32) for block in range(9)]
    for start, count, block in (
        (UP, 4, 1), (UP_LEFT, 1, 0), (UP_RIGHT, 1, 2), (DOWN, 4, 7), (DOWN_LEFT, 1, 6), (DOWN_RIGHT, 1, 8),
        (WEST, 4, 3), (EAST, 4, 5),
    ):
        mask[8 * start:8 * (start + count), :] = jnp.full((8 * count, CELLS), live[block], F32)

    pair.wait_recv()
    tchip[...] = (tpart[core] + tsib[...]).reshape(n_x, owned, 8, HDIM)
    for step in range(1, n_x):
        to = (x + step) % n_x
        remote(tchip.at[to], xin.at[step - 1], x_send.at[0], x_recv.at[0], ha=2 * to + core).start()

    def rim_grads(part, chunk):
        low, high = PARTS[part]
        rows = 8 * (high - low)
        lanes = lanes_of(chunk)
        wait_bytes(halo.at[:, low:high, :, lanes], halo_recv.at[part, chunk])
        for head in range(chunk * PER_CHUNK, (chunk + 1) * PER_CHUNK):
            at = pl.ds(head * HDIM, HDIM)
            key, value = (halo[kind, low:high, :, at].reshape(rows, HDIM) for kind in range(2))
            probs, score_grad = score_grads(
                key, value, q[:, at], o[:, at], *statistics(head), mask[8 * low:8 * high, :]
            )
            rim[0, low:high, :, at] = dot(score_grad, q[:, at], NN).reshape(high - low, 8, HDIM)
            rim[1, low:high, :, at] = dot(probs, o[:, at], NN).reshape(high - low, 8, HDIM)
            query_part = dot(score_grad, key, TN)
            dq[:, at] = query_part if part == 0 else dq[:, at] + query_part

    def corners_out(side, chunk):
        lanes = lanes_of(chunk)
        for source, start, where in ((0, (UP_RIGHT, UP_LEFT)[side], up), (1, (DOWN_RIGHT, DOWN_LEFT)[side], down)):
            remote(
                rim.at[:, start, :, lanes], corner_in.at[side, source, :, :, lanes],
                corner_send.at[side, chunk], corner_recv.at[side, chunk], ha=where,
            ).start()

    def cols_out(side, chunk):
        lanes = lanes_of(chunk)
        wait_bytes(corner_in.at[side, :, :, :, lanes], corner_recv.at[side, chunk])
        start, where = ((EAST, right), (WEST, left))[side]
        below, above = ((start, start + 3), (start + 3, start))[side]
        rim[:, below, :, lanes] += corner_in[side, 0, :, :, lanes]
        rim[:, above, :, lanes] += corner_in[side, 1, :, :, lanes]
        remote(
            rim.at[:, start:start + 4, :, lanes], cols_in.at[side, :, :, :, lanes],
            cols_send.at[side, chunk], cols_recv.at[side, chunk], wa=where,
        ).start()

    def rows_out(chunk):
        lanes = lanes_of(chunk)
        for source, start, where in ((0, UP, up), (1, DOWN, down)):
            remote(
                rim.at[:, start:start + 4, :, lanes], rows_in.at[source, :, :, :, lanes],
                rows_send.at[chunk], rows_recv.at[chunk], ha=where,
            ).start()

    for chunk in range(CHUNKS):
        rim_grads(0, chunk)
        corners_out(0, chunk)

    pl.when(wa == 0)(send_west)

    for chunk in range(CHUNKS):
        cols_out(0, chunk)
    for chunk in range(CHUNKS):
        rim_grads(1, chunk)
        rows_out(chunk)

    wait_bytes(xin, x_recv.at[0])
    total = tchip[x]
    for step in range(n_x - 1):
        total = total + xin[step]
    zpart[...] = total

    @pl.when(wa != 0)
    def _():
        remote(zpart, zin.at[wa - 1], z_send.at[0], z_recv.at[0], wa=0).start()

    for head in range(HEADS):
        at = pl.ds(head * HDIM, HDIM)
        probs, score_grad = score_grads(own[0, :, at], own[1, :, at], q[:, at], o[:, at], *statistics(head), live[4])
        acc[0, :, :, at] = dot(score_grad, q[:, at], NN).reshape(CELLS // 8, 8, HDIM)
        acc[1, :, :, at] = dot(probs, o[:, at], NN).reshape(CELLS // 8, 8, HDIM)
        dq[:, at] += dot(score_grad, own[0, :, at], TN) + dot(text_grad[head], tk[:, at], TN)

    for chunk in range(CHUNKS):
        rim_grads(2, chunk)
        corners_out(1, chunk)
    for chunk in range(CHUNKS):
        cols_out(1, chunk)

    def gather_x():
        tfin[core, x] = zall[...]
        for step in range(1, n_x):
            to = (x + step) % n_x
            remote(zall, tfin.at[core, x], xa_send.at[0], xa_recv.at[0], ha=2 * to + core).start()

    @pl.when(wa == 0)
    def _():
        wait_bytes(zin, z_recv.at[0])
        final = zpart[...]
        for col in range(n_wa - 1):
            final = final + zin[col]
        zall[...] = final.astype(BF16)
        gather_x()
        for col in range(1, n_wa):
            remote(zall, zall, za_send.at[0], za_recv.at[0], wa=col).start()

    dq_out[...] = (dq[...] * SCALE).astype(BF16)

    @pl.when(wa != 0)
    def _():
        wait_bytes(zall, za_recv.at[0])
        gather_x()

    for chunk in range(CHUNKS):
        lanes = lanes_of(chunk)
        wait_bytes(rows_in.at[:, :, :, :, lanes], rows_recv.at[chunk])
        acc[:, BOTTOM:BOTTOM + 4, :, lanes] += rows_in[0, :, :, :, lanes]
        acc[:, TOP:TOP + 4, :, lanes] += rows_in[1, :, :, :, lanes]
        wait_bytes(cols_in.at[1, :, :, :, lanes], cols_recv.at[1, chunk])
        acc[:, RIGHT:RIGHT + 4, :, lanes] += cols_in[1, :, :, :, lanes]
        wait_bytes(cols_in.at[0, :, :, :, lanes], cols_recv.at[0, chunk])
        acc[:, LEFT:LEFT + 3, :, lanes] += cols_in[0, :, 0:3, :, lanes]
        acc[:, TOP, :, lanes] += cols_in[0, :, 3, :, lanes]
        for at, out, factor in ((0, dk_out, SCALE), (1, dv_out, 1.0)):
            total = (acc[at, :, :, lanes] * factor).reshape(CELLS, LANES).astype(BF16)
            out[:, lanes] = dot(back[...], total, NN).astype(BF16)

    wait_bytes(tfin.at[core, 0:n_x - 1], xa_recv.at[0])
    last = remote(tfin.at[core], tfin.at[core], pair_send.at[1], pair_recv.at[1], ha=sibling)
    last.start()
    wait_bytes(tfin.at[1 - core], pair_recv.at[1])
    for at in range(2):
        for tile in range(TILES):
            text_out[at, tile % 4, :, (tile // 4) * HDIM:(tile // 4 + 1) * HDIM] = tfin[at, tile // owned, tile % owned]

    last.wait_send()
    pair.wait_send()
    for chunk in range(CHUNKS):
        lanes = lanes_of(chunk)
        for part, (low, high) in enumerate(PARTS):
            wait_bytes(halo.at[:, low:high, :, lanes], halo_send.at[part, chunk])
        wait_bytes(rows_in.at[:, :, :, :, lanes], rows_send.at[chunk])
        for side in range(2):
            wait_bytes(corner_in.at[side, :, :, :, lanes], corner_send.at[side, chunk])
            wait_bytes(cols_in.at[side, :, :, :, lanes], cols_send.at[side, chunk])
    wait_bytes(xin, x_send.at[0])

    @pl.when(wa != 0)
    def _():
        wait_bytes(zpart, z_send.at[0])

    @pl.when(wa == 0)
    def _():
        wait_bytes(zin.at[:, :, 0:4, :], za_send.at[0])

    wait_bytes(tfin.at[core, 0:n_x - 1], xa_send.at[0])


def store(dq, dk, dv, text, dq_hbm, dk_hbm, dv_hbm, dtk_hbm, dtv_hbm, sem):
    copies = [
        pltpu.make_async_copy(src, dst, sem.at[at])
        for at, (src, dst) in enumerate((
            (dq, dq_hbm), (dk, dk_hbm), (dv, dv_hbm), (text.at[0], dtk_hbm), (text.at[1], dtv_hbm),
        ))
    ]
    for copy in copies:
        copy.start()
    for copy in copies:
        copy.wait()


def local(n_ha, n_wa, queries, keys, values, out_grad, log_norm, delta_rows, text_keys, text_values, window_table):
    n_x = n_ha // 2
    owned = TILES // n_x
    rows = region_rows()
    order = np.zeros((8 * (LAST + 1), CELLS), np.float32)
    order[np.arange(len(rows)), rows] = 1.0
    back = order[:CELLS].T
    hbm = pl.BlockSpec(memory_space=pl.ANY)
    vmem = pltpu.VMEM
    dma = pltpu.SemaphoreType.DMA
    flat = (CELLS, WIDTH)
    outs = pl.pallas_call(
        functools.partial(kernel, n_ha, n_wa),
        out_shape=[vmem(flat, BF16)] * 3 + [vmem((2, TEXT // 8, 8, WIDTH), BF16)],
        in_specs=[hbm] * 11,
        out_specs=[pl.BlockSpec(memory_space=vmem)] * 4,
        scratch_shapes=[
            vmem(flat, BF16), vmem(flat, BF16), vmem(flat, BF16), vmem(flat, BF16),
            vmem((CELLS, HEADS), F32), vmem((CELLS, HEADS), F32),
            vmem((TEXT, WIDTH), BF16), vmem((TEXT, WIDTH), BF16),
            vmem((8 * (LAST + 1), CELLS), BF16), vmem((CELLS, CELLS), BF16),
            pltpu.SMEM((window_table.shape[2],) + window_table.shape[:2], jnp.int32),
            vmem((16, CELLS), F32), vmem((16, CELLS), F32), vmem((8 * BORROWED, CELLS), F32),
            vmem((2, LAST + 1, 8, WIDTH), BF16), vmem((2, CELLS, WIDTH), BF16),
            vmem((2, BORROWED, 8, WIDTH), BF16), vmem((2, BORROWED, 8, WIDTH), F32),
            vmem((2, 2, 4, 8, WIDTH), F32), vmem((2, 2, 2, 8, WIDTH), F32), vmem((2, 2, 4, 8, WIDTH), F32),
            vmem((2, CELLS // 8, 8, WIDTH), F32), vmem(flat, F32), vmem((HEADS, TEXT, CELLS), BF16),
            vmem((2, TILES, 8, HDIM), F32), vmem((TILES, 8, HDIM), F32), vmem((n_x, owned, 8, HDIM), F32),
            vmem((n_x - 1, owned, 8, HDIM), F32), vmem((owned, 8, HDIM), F32), vmem((n_wa - 1, owned, 8, HDIM), F32),
            vmem((owned, 8, HDIM), BF16), vmem((2, n_x, owned, 8, HDIM), BF16),
            dma((11,)), dma((3, CHUNKS)), dma((3, CHUNKS)), dma((CHUNKS,)), dma((CHUNKS,)),
            dma((2, CHUNKS)), dma((2, CHUNKS)), dma((2, CHUNKS)), dma((2, CHUNKS)),
            dma((2,)), dma((2,)), dma((1,)), dma((1,)), dma((1,)), dma((1,)),
            dma((1,)), dma((1,)), dma((1,)), dma((1,)), pltpu.SemaphoreType.REGULAR((2,)),
        ],
        compiler_params=pltpu.CompilerParams(collective_id=0, has_side_effects=True, vmem_limit_bytes=56 << 20),
    )(
        queries.reshape(flat), keys.reshape(flat), values.reshape(flat), out_grad.reshape(flat),
        log_norm.transpose(1, 2, 3, 0).reshape(CELLS, HEADS), delta_rows.transpose(1, 2, 3, 0).reshape(CELLS, HEADS),
        text_keys, text_values, window_table.transpose(2, 0, 1),
        jnp.asarray(order, BF16), jnp.asarray(back, BF16),
    )
    outs = pl.pallas_call(
        store,
        out_shape=[jax.ShapeDtypeStruct(flat, BF16)] * 3 + [jax.ShapeDtypeStruct((TEXT // 8, 8, WIDTH), BF16)] * 2,
        in_specs=[pl.BlockSpec(memory_space=vmem)] * 4,
        out_specs=[hbm] * 5,
        scratch_shapes=[dma((5,))],
        compiler_params=pltpu.CompilerParams(has_side_effects=True, vmem_limit_bytes=1 << 20),
    )(*outs)
    cells = queries.shape
    return (
        outs[0].reshape(cells), outs[1].reshape(cells), outs[2].reshape(cells),
        outs[3].reshape(TEXT, WIDTH), outs[4].reshape(TEXT, WIDTH),
    )


def solution(mesh):
    cells = P("group", "ha", "wa", None)
    stats = P(None, "group", "ha", "wa")
    text = P("group", None)
    return jax.shard_map(
        functools.partial(local, mesh.shape["ha"], mesh.shape["wa"]),
        mesh=mesh,
        in_specs=(cells, cells, cells, cells, stats, stats, text, text, P()),
        out_specs=(cells, cells, cells, text, text),
        check_vma=False,
    )
```

time: 78.9 us -> 88.8 us (1.13)
  the two profiles are of different devices: /device:TPU:209 before, /device:TPU:65 now
where the time goes in v2:
time: 88.8 us; the launch traced here: 88.6 us
  Pallas kernels  88 us (99%)
    pallas_call x1, Pallas kernels, local(): pl.pallas_call(functools.partial(kernel, n_ha, n_wa), out_shape=[vmem(fla...  86.9 us

profile of v2, /device:TPU:65, one launch (start us, length us, event | category | flops | bytes accessed | tf_op | source)
XLA Modules:
  0.0 88.6 jit_solution(7905036325848875830)
XLA Ops:
  0.6 86.9 %shard_map.146 = (bf16[128,1536]{1,0:T(8,128)(2,1)S(1)}, bf16[128,1536]{1,0:T(8,128)(2,1)S(1)}, bf16[128,1536]{1,0:T(8,128)(2,1)S(1)}, bf16[2,4,8,1536]{3,2,1,0:T(8,128)(2,1)S(1)}) custom-call(bf16[128,1536]{1,0:T(8,128)(2,1)} %bitcast.16, bf16[128,1536]{1,0:T(8,128)(2,1)} %bitcast.17, bf16[128,1536]{1,0:T(8,128)(2,1)} %bitcast.18, ...), custom_call_target="tpu_custom_call" | custom-call | tf_op jit(solution)/shard_map/pallas_call | solution.py:376
  87.5 1.1 %shard_map.147 = (bf16[128,1536]{1,0:T(8,128)(2,1)}, bf16[128,1536]{1,0:T(8,128)(2,1)}, bf16[128,1536]{1,0:T(8,128)(2,1)}, bf16[4,8,1536]{2,1,0:T(8,128)(2,1)}, bf16[4,8,1536]{2,1,0:T(8,128)(2,1)}) custom-call(bf16[128,1536]{1,0:T(8,128)(2,1)S(1)} %get-tuple-element.14.dq, bf16[128,1536]{1,0:T(8,128)(2,1)S(1)} %get-tuple-element.15.dk, ...), custom_call_target="tpu_custom_call" | custom-call | tf_op jit(solution)/shard_map/pallas_call | solution.py:407

commit v3 on v2

--- a/solution.py
+++ b/solution.py
@@ -66,10 +66,10 @@
     q_hbm, k_hbm, v_hbm, o_hbm, norm_hbm, delta_hbm, tk_hbm, tv_hbm, table_hbm, order_hbm, back_hbm,
     dq_out, dk_out, dv_out, text_out,
     q, k, v, o, norm12, delta12, tk, tv, order, back, table,
-    norm, delta, mask, packed, own, halo, rim, rows_in, corner_in, cols_in, acc, dq, text_grad,
+    norm, delta, mask, packed, own, halo, rim, rows_in, corner_in, cols_in, acc, grads,
     tpart, tsib, tchip, xin, zpart, zin, zall, tfin,
     load_sem, halo_send, halo_recv, rows_send, rows_recv, corner_send, corner_recv, cols_send, cols_recv,
-    pair_send, pair_recv, x_send, x_recv, z_send, z_recv, za_send, za_recv, xa_send, xa_recv, ready,
+    pair_send, pair_recv, x_send, x_recv, z_send, z_recv, za_send, za_recv, xa_send, xa_recv, ready, met,
 ):
     n_x = n_ha // 2
     owned = TILES // n_x
@@ -78,6 +78,13 @@
     up, down = (ha + n_ha - 1) % n_ha, (ha + 1) % n_ha
     left, right = (wa + n_wa - 1) % n_wa, (wa + 1) % n_wa
     sibling = 2 * x + 1 - core
+    distances = [2 ** at for at in range((n_ha // 4).bit_length())]
+    far_first = sorted(range(1, n_x), key=lambda step: -min(step, n_x - step))
+    half, helper = n_wa // 2, n_wa // 4 + 1
+    corner_device = (wa == 0) & (ha == 0)
+    first_owner = (wa == 0) & (ha != 0)
+    is_owner = first_owner | (wa == 1)
+    greeters = jnp.where(ha == 0, 1, 2) - jnp.where(is_owner, 1, 0)
 
     def remote(src, dst, send, recv, **where):
         return pltpu.make_async_remote_copy(
@@ -101,8 +108,11 @@
         signal(barrier, ha=down, wa=col)
     signal(barrier, ha=up)
     signal(barrier, ha=down)
-    for step in range(1, n_x):
-        signal(barrier, ha=(ha + 2 * step) % n_ha)
+
+    @pl.when(wa != 0)
+    def _():
+        for step in range(1, n_x):
+            signal(barrier, ha=(ha + 2 * step) % n_ha)
 
     loads = [
         pltpu.make_async_copy(src, dst, load_sem.at[at])
@@ -114,10 +124,13 @@
     for load in loads:
         load.start()
 
-    @pl.when(wa == 0)
-    def _():
-        for col in range(1, n_wa):
-            signal(barrier, wa=col)
+    for owner, cond in ((0, first_owner), (1, wa == 1)):
+
+        @pl.when(cond)
+        def _():
+            for col in range(n_wa):
+                if col != owner:
+                    signal(barrier, wa=col)
 
     def send_halo(part, chunk, sends):
         lanes = lanes_of(chunk)
@@ -129,7 +142,13 @@
             ).start()
 
     def enter():
-        pl.semaphore_wait(barrier, 5 + n_x - 1 + jnp.where(wa == 0, 0, 1))
+        pl.semaphore_wait(barrier, 5 + greeters + jnp.where(wa == 0, 0, n_x - 1))
+
+        @pl.when(wa == 0)
+        def _():
+            signal(met.at[0], ha=up)
+            signal(met.at[0], ha=down)
+
         signal(ready.at[0], wa=right)
         signal(ready.at[1], ha=up, wa=right)
         signal(ready.at[1], ha=down, wa=right)
@@ -139,18 +158,32 @@
                 (RIGHT, DOWN_LEFT, 1, {"ha": up, "wa": right}),
                 (BOTTOM, UP_LEFT, 1, {"ha": down, "wa": right}),
             ))
+
+    def meet_row(at):
+        pl.semaphore_wait(met.at[at], 2)
+        if at + 1 < len(distances):
+            signal(met.at[at + 1], ha=(ha + distances[at + 1]) % n_ha)
+            signal(met.at[at + 1], ha=(ha + n_ha - distances[at + 1]) % n_ha)
+
+    def send_rows():
+        for chunk in range(CHUNKS):
             send_halo(1, chunk, ((TOP, DOWN, 4, {"ha": up}), (BOTTOM, UP, 4, {"ha": down})))
 
-    def send_west():
+    def send_west(together):
+        side = ((LEFT, EAST, 4, {"wa": left}),)
+        corners = (
+            (TOP, DOWN_RIGHT, 1, {"ha": up, "wa": left}),
+            (LEFT, UP_RIGHT, 1, {"ha": down, "wa": left}),
+        )
         pl.semaphore_wait(ready.at[0], 1)
+        if together:
+            pl.semaphore_wait(ready.at[1], 2)
         for chunk in range(CHUNKS):
-            send_halo(2, chunk, ((LEFT, EAST, 4, {"wa": left}),))
-        pl.semaphore_wait(ready.at[1], 2)
-        for chunk in range(CHUNKS):
-            send_halo(2, chunk, (
-                (TOP, DOWN_RIGHT, 1, {"ha": up, "wa": left}),
-                (LEFT, UP_RIGHT, 1, {"ha": down, "wa": left}),
-            ))
+            send_halo(2, chunk, side + corners if together else side)
+        if not together:
+            pl.semaphore_wait(ready.at[1], 2)
+            for chunk in range(CHUNKS):
+                send_halo(2, chunk, corners)
 
     for load in loads[0:3]:
         load.wait()
@@ -160,7 +193,7 @@
             packed[at, :, :, lanes_of(chunk)] = moved.reshape(LAST + 1, 8, LANES).astype(BF16)
             own[at, :, lanes_of(chunk)] = moved[0:CELLS].astype(BF16)
 
-    late = (wa == n_wa - 1) | ((wa == 0) & (ha == 0))
+    late = (wa == n_wa - 1) | corner_device
     pl.when(late)(enter)
 
     for load, src, dst in ((loads[3], norm12, norm), (loads[4], delta12, delta)):
@@ -175,16 +208,9 @@
     for head in range(HEADS):
         at = pl.ds(head * HDIM, HDIM)
         probs, score_grad = score_grads(tk[:, at], tv[:, at], q[:, at], o[:, at], *statistics(head), None)
-        text_grad[head] = score_grad
+        grads[head, 0:TEXT] = score_grad
         tpart[0, 4 * head:4 * head + 4] = (dot(score_grad, q[:, at], NN) * SCALE).reshape(4, 8, HDIM)
         tpart[1, 4 * head:4 * head + 4] = dot(probs, o[:, at], NN).reshape(4, 8, HDIM)
-
-    pl.when(jnp.logical_not(late))(enter)
-
-    pair = remote(tpart.at[1 - core], tsib, pair_send.at[0], pair_recv.at[0], ha=sibling)
-    pair.start()
-
-    pl.when(wa != 0)(send_west)
 
     for load in loads[9:11]:
         load.wait()
@@ -195,11 +221,42 @@
     ):
         mask[8 * start:8 * (start + count), :] = jnp.full((8 * count, CELLS), live[block], F32)
 
+    def own_grads():
+        for head in range(HEADS):
+            at = pl.ds(head * HDIM, HDIM)
+            probs, score_grad = score_grads(own[0, :, at], own[1, :, at], q[:, at], o[:, at], *statistics(head), live[4])
+            acc[0, :, :, at] = dot(score_grad, q[:, at], NN).reshape(CELLS // 8, 8, HDIM)
+            acc[1, :, :, at] = dot(probs, o[:, at], NN).reshape(CELLS // 8, 8, HDIM)
+            grads[head, TEXT:TEXT + CELLS] = score_grad
+
+    @pl.when(jnp.logical_not(late))
+    def _():
+        own_grads()
+        enter()
+
+    pair = remote(tpart.at[1 - core], tsib, pair_send.at[0], pair_recv.at[0], ha=sibling)
+    pair.start()
+
+    pl.when(jnp.logical_not(late))(send_rows)
+    pl.when((wa >= 2) & (wa != n_wa - 1))(lambda: send_west(False))
+
+    @pl.when(wa == 0)
+    def _():
+        for at in range(len(distances) - 1):
+            meet_row(at)
+        pl.when(first_owner)(lambda: send_west(True))
+        meet_row(len(distances) - 1)
+
     pair.wait_recv()
     tchip[...] = (tpart[core] + tsib[...]).reshape(n_x, owned, 8, HDIM)
-    for step in range(1, n_x):
+    for step in far_first:
         to = (x + step) % n_x
         remote(tchip.at[to], xin.at[step - 1], x_send.at[0], x_recv.at[0], ha=2 * to + core).start()
+
+    @pl.when(corner_device)
+    def _():
+        send_rows()
+        send_west(True)
 
     def rim_grads(part, chunk):
         low, high = PARTS[part]
@@ -214,8 +271,7 @@
             )
             rim[0, low:high, :, at] = dot(score_grad, q[:, at], NN).reshape(high - low, 8, HDIM)
             rim[1, low:high, :, at] = dot(probs, o[:, at], NN).reshape(high - low, 8, HDIM)
-            query_part = dot(score_grad, key, TN)
-            dq[:, at] = query_part if part == 0 else dq[:, at] + query_part
+            grads[head, TEXT + CELLS + 8 * low:TEXT + CELLS + 8 * high] = score_grad
 
     def corners_out(side, chunk):
         lanes = lanes_of(chunk)
@@ -245,64 +301,111 @@
                 rows_send.at[chunk], rows_recv.at[chunk], ha=where,
             ).start()
 
+    def sum_x():
+        wait_bytes(xin, x_recv.at[0])
+        total = tchip[x]
+        for step in range(n_x - 1):
+            total = total + xin[step]
+        zpart[...] = total
+        for at, cond in enumerate(((wa != 0) & (ha != 0), wa != 1)):
+
+            @pl.when(cond)
+            def _():
+                remote(zpart, zin.at[wa], z_send.at[at], z_recv.at[0], wa=at).start()
+
+    pl.when(jnp.logical_not(late) & (wa != 0))(sum_x)
+
     for chunk in range(CHUNKS):
+        if chunk == CHUNKS - 1:
+
+            @pl.when(late)
+            def _():
+                sum_x()
+                cols_out(0, 0)
+
         rim_grads(0, chunk)
         corners_out(0, chunk)
 
-    pl.when(wa == 0)(send_west)
-
-    for chunk in range(CHUNKS):
-        cols_out(0, chunk)
+    def east_cols(start):
+        for chunk in range(start, CHUNKS):
+            cols_out(0, chunk)
+
+    def west_cols():
+        for chunk in range(CHUNKS):
+            cols_out(1, chunk)
+
+    pl.when(wa == n_wa - 1)(send_rows)
+    pl.when(jnp.logical_not(late | first_owner))(lambda: east_cols(0))
+
+    @pl.when(late)
+    def _():
+        east_cols(1)
+        own_grads()
+
+    pl.when(wa == n_wa - 1)(lambda: send_west(False))
+
     for chunk in range(CHUNKS):
         rim_grads(1, chunk)
         rows_out(chunk)
 
-    wait_bytes(xin, x_recv.at[0])
-    total = tchip[x]
-    for step in range(n_x - 1):
-        total = total + xin[step]
-    zpart[...] = total
-
-    @pl.when(wa != 0)
-    def _():
-        remote(zpart, zin.at[wa - 1], z_send.at[0], z_recv.at[0], wa=0).start()
-
-    for head in range(HEADS):
-        at = pl.ds(head * HDIM, HDIM)
-        probs, score_grad = score_grads(own[0, :, at], own[1, :, at], q[:, at], o[:, at], *statistics(head), live[4])
-        acc[0, :, :, at] = dot(score_grad, q[:, at], NN).reshape(CELLS // 8, 8, HDIM)
-        acc[1, :, :, at] = dot(probs, o[:, at], NN).reshape(CELLS // 8, 8, HDIM)
-        dq[:, at] += dot(score_grad, own[0, :, at], TN) + dot(text_grad[head], tk[:, at], TN)
+    @pl.when(first_owner)
+    def _():
+        sum_x()
+        east_cols(0)
+
+    pl.when(wa == 1)(lambda: send_west(False))
 
     for chunk in range(CHUNKS):
         rim_grads(2, chunk)
         corners_out(1, chunk)
-    for chunk in range(CHUNKS):
-        cols_out(1, chunk)
+
+    west_cols()
 
     def gather_x():
         tfin[core, x] = zall[...]
-        for step in range(1, n_x):
+        for step in far_first:
             to = (x + step) % n_x
             remote(zall, tfin.at[core, x], xa_send.at[0], xa_recv.at[0], ha=2 * to + core).start()
 
-    @pl.when(wa == 0)
-    def _():
-        wait_bytes(zin, z_recv.at[0])
-        final = zpart[...]
-        for col in range(n_wa - 1):
+    @pl.when(is_owner)
+    def _():
+        zin[wa] = zpart[...]
+        wait_bytes(zin.at[0:n_wa - 1], z_recv.at[0])
+        final = zin[0]
+        for col in range(1, n_wa):
             final = final + zin[col]
         zall[...] = final.astype(BF16)
         gather_x()
-        for col in range(1, n_wa):
-            remote(zall, zall, za_send.at[0], za_recv.at[0], wa=col).start()
-
-    dq_out[...] = (dq[...] * SCALE).astype(BF16)
-
-    @pl.when(wa != 0)
+
+    served = (
+        (first_owner, range(half + 2, n_wa), 0),
+        ((wa == 1) & (ha != 0), range(2, half + 2), 0),
+        ((wa == 1) & (ha == 0), range(2, half + 2), n_x),
+        ((wa == helper) & (ha == 0), range(half + 2, n_wa), 0),
+    )
+    for cond, cols, rows in served[:3]:
+
+        @pl.when(cond)
+        def _():
+            for to in range(rows):
+                remote(zall, tfin.at[core, x], za_send.at[0], xa_recv.at[0], ha=2 * to, wa=0).start()
+            for col in cols:
+                remote(zall, zall, za_send.at[0], za_recv.at[0], wa=col).start()
+
+    @pl.when(wa >= 2)
     def _():
         wait_bytes(zall, za_recv.at[0])
         gather_x()
+
+    @pl.when(served[3][0])
+    def _():
+        for col in served[3][1]:
+            remote(zall, zall, za_send.at[0], za_recv.at[0], wa=col).start()
+
+    for head in range(HEADS):
+        at = pl.ds(head * HDIM, HDIM)
+        keys = jnp.concatenate((tk[:, at], own[0, :, at], halo[0, :, :, at].reshape(8 * BORROWED, HDIM)), axis=0)
+        dq_out[:, at] = (dot(grads[head], keys, TN) * SCALE).astype(BF16)
 
     for chunk in range(CHUNKS):
         lanes = lanes_of(chunk)
@@ -318,7 +421,14 @@
             total = (acc[at, :, :, lanes] * factor).reshape(CELLS, LANES).astype(BF16)
             out[:, lanes] = dot(back[...], total, NN).astype(BF16)
 
-    wait_bytes(tfin.at[core, 0:n_x - 1], xa_recv.at[0])
+    @pl.when(corner_device)
+    def _():
+        wait_bytes(tfin.at[core], xa_recv.at[0])
+
+    @pl.when(jnp.logical_not(corner_device))
+    def _():
+        wait_bytes(tfin.at[core, 0:n_x - 1], xa_recv.at[0])
+
     last = remote(tfin.at[core], tfin.at[core], pair_send.at[1], pair_recv.at[1], ha=sibling)
     last.start()
     wait_bytes(tfin.at[1 - core], pair_recv.at[1])
@@ -338,15 +448,21 @@
             wait_bytes(cols_in.at[side, :, :, :, lanes], cols_send.at[side, chunk])
     wait_bytes(xin, x_send.at[0])
 
-    @pl.when(wa != 0)
-    def _():
-        wait_bytes(zpart, z_send.at[0])
-
-    @pl.when(wa == 0)
-    def _():
-        wait_bytes(zin.at[:, :, 0:4, :], za_send.at[0])
-
-    wait_bytes(tfin.at[core, 0:n_x - 1], xa_send.at[0])
+    for at, cond in enumerate(((wa != 0) & (ha != 0), wa != 1)):
+
+        @pl.when(cond)
+        def _():
+            wait_bytes(zpart, z_send.at[at])
+
+    for cond, cols, rows in served:
+
+        @pl.when(cond)
+        def _():
+            wait_bytes(zin.at[0:(len(cols) + rows) // 2], za_send.at[0])
+
+    @pl.when(jnp.logical_not(corner_device))
+    def _():
+        wait_bytes(tfin.at[core, 0:n_x - 1], xa_send.at[0])
 
 
 def store(dq, dk, dv, text, dq_hbm, dk_hbm, dv_hbm, dtk_hbm, dtv_hbm, sem):
@@ -388,14 +504,14 @@
             vmem((2, LAST + 1, 8, WIDTH), BF16), vmem((2, CELLS, WIDTH), BF16),
             vmem((2, BORROWED, 8, WIDTH), BF16), vmem((2, BORROWED, 8, WIDTH), F32),
             vmem((2, 2, 4, 8, WIDTH), F32), vmem((2, 2, 2, 8, WIDTH), F32), vmem((2, 2, 4, 8, WIDTH), F32),
-            vmem((2, CELLS // 8, 8, WIDTH), F32), vmem(flat, F32), vmem((HEADS, TEXT, CELLS), BF16),
+            vmem((2, CELLS // 8, 8, WIDTH), F32), vmem((HEADS, TEXT + CELLS + 8 * BORROWED, CELLS), BF16),
             vmem((2, TILES, 8, HDIM), F32), vmem((TILES, 8, HDIM), F32), vmem((n_x, owned, 8, HDIM), F32),
-            vmem((n_x - 1, owned, 8, HDIM), F32), vmem((owned, 8, HDIM), F32), vmem((n_wa - 1, owned, 8, HDIM), F32),
+            vmem((n_x - 1, owned, 8, HDIM), F32), vmem((owned, 8, HDIM), F32), vmem((n_wa, owned, 8, HDIM), F32),
             vmem((owned, 8, HDIM), BF16), vmem((2, n_x, owned, 8, HDIM), BF16),
             dma((11,)), dma((3, CHUNKS)), dma((3, CHUNKS)), dma((CHUNKS,)), dma((CHUNKS,)),
             dma((2, CHUNKS)), dma((2, CHUNKS)), dma((2, CHUNKS)), dma((2, CHUNKS)),
-            dma((2,)), dma((2,)), dma((1,)), dma((1,)), dma((1,)), dma((1,)),
-            dma((1,)), dma((1,)), dma((1,)), dma((1,)), pltpu.SemaphoreType.REGULAR((2,)),
+            dma((2,)), dma((2,)), dma((1,)), dma((1,)), dma((2,)), dma((1,)),
+            dma((1,)), dma((1,)), dma((1,)), dma((1,)), pltpu.SemaphoreType.REGULAR((2,)), pltpu.SemaphoreType.REGULAR(((n_ha // 4).bit_length(),)),
         ],
         compiler_params=pltpu.CompilerParams(collective_id=0, has_side_effects=True, vmem_limit_bytes=56 << 20),
     )(

time: 88.8 us -> 77.6 us (0.87)
  Pallas kernels: 88 us -> 76.8 us
    pallas_call x1, Pallas kernels: 86.9 us -> 75.7 us  [local(): pl.pallas_call(functools.partial(kernel, n_ha, n_wa), out_shape=[vmem(fla...]
where the time goes in v3:
time: 77.6 us; the launch traced here: 77.5 us
  Pallas kernels  76.8 us (99%)
    pallas_call x1, Pallas kernels, local(): pl.pallas_call(functools.partial(kernel, n_ha, n_wa), out_shape=[vmem(fla...  75.7 us

profile of v3, /device:TPU:65, one launch (start us, length us, event | category | flops | bytes accessed | tf_op | source)
XLA Modules:
  0.0 77.5 jit_solution(99152744066652475)
XLA Ops:
  0.6 75.7 %shard_map.146 = (bf16[128,1536]{1,0:T(8,128)(2,1)S(1)}, bf16[128,1536]{1,0:T(8,128)(2,1)S(1)}, bf16[128,1536]{1,0:T(8,128)(2,1)S(1)}, bf16[2,4,8,1536]{3,2,1,0:T(8,128)(2,1)S(1)}) custom-call(bf16[128,1536]{1,0:T(8,128)(2,1)} %bitcast.16, bf16[128,1536]{1,0:T(8,128)(2,1)} %bitcast.17, bf16[128,1536]{1,0:T(8,128)(2,1)} %bitcast.18, ...), custom_call_target="tpu_custom_call" | custom-call | tf_op jit(solution)/shard_map/pallas_call | solution.py:492
  76.4 1.1 %shard_map.147 = (bf16[128,1536]{1,0:T(8,128)(2,1)}, bf16[128,1536]{1,0:T(8,128)(2,1)}, bf16[128,1536]{1,0:T(8,128)(2,1)}, bf16[4,8,1536]{2,1,0:T(8,128)(2,1)}, bf16[4,8,1536]{2,1,0:T(8,128)(2,1)}) custom-call(bf16[128,1536]{1,0:T(8,128)(2,1)S(1)} %get-tuple-element.14.dq, bf16[128,1536]{1,0:T(8,128)(2,1)S(1)} %get-tuple-element.15.dk, ...), custom_call_target="tpu_custom_call" | custom-call | tf_op jit(solution)/shard_map/pallas_call | solution.py:523

commit v4 on v3

--- a/solution.py
+++ b/solution.py
@@ -17,7 +17,7 @@
 WIDTH = HEADS * HDIM
 CELLS = FRAMES * TILE * TILE
 TEXT = 32
-CHUNKS = 3
+CHUNKS = 2
 PER_CHUNK = HEADS // CHUNKS
 LANES = PER_CHUNK * HDIM
 TILES = HEADS * TEXT // 8
@@ -101,19 +101,6 @@
     def lanes_of(chunk):
         return pl.ds(chunk * LANES, LANES)
 
-    barrier = pltpu.get_barrier_semaphore()
-    for col in (left,):
-        signal(barrier, wa=col)
-        signal(barrier, ha=up, wa=col)
-        signal(barrier, ha=down, wa=col)
-    signal(barrier, ha=up)
-    signal(barrier, ha=down)
-
-    @pl.when(wa != 0)
-    def _():
-        for step in range(1, n_x):
-            signal(barrier, ha=(ha + 2 * step) % n_ha)
-
     loads = [
         pltpu.make_async_copy(src, dst, load_sem.at[at])
         for at, (src, dst) in enumerate((
@@ -124,6 +111,19 @@
     for load in loads:
         load.start()
 
+    barrier = pltpu.get_barrier_semaphore()
+    for col in (left,):
+        signal(barrier, wa=col)
+        signal(barrier, ha=up, wa=col)
+        signal(barrier, ha=down, wa=col)
+    signal(barrier, ha=up)
+    signal(barrier, ha=down)
+
+    @pl.when(wa != 0)
+    def _():
+        for step in range(1, n_x):
+            signal(barrier, ha=(ha + 2 * step) % n_ha)
+
     for owner, cond in ((0, first_owner), (1, wa == 1)):
 
         @pl.when(cond)
@@ -154,10 +154,11 @@
         signal(ready.at[1], ha=down, wa=right)
         for chunk in range(CHUNKS):
             send_halo(0, chunk, (
-                (RIGHT, WEST, 4, {"wa": right}),
                 (RIGHT, DOWN_LEFT, 1, {"ha": up, "wa": right}),
                 (BOTTOM, UP_LEFT, 1, {"ha": down, "wa": right}),
             ))
+        for chunk in range(CHUNKS):
+            send_halo(0, chunk, ((RIGHT, WEST, 4, {"wa": right}),))
 
     def meet_row(at):
         pl.semaphore_wait(met.at[at], 2)
@@ -179,7 +180,7 @@
         if together:
             pl.semaphore_wait(ready.at[1], 2)
         for chunk in range(CHUNKS):
-            send_halo(2, chunk, side + corners if together else side)
+            send_halo(2, chunk, corners + side if together else side)
         if not together:
             pl.semaphore_wait(ready.at[1], 2)
             for chunk in range(CHUNKS):
@@ -330,10 +331,6 @@
         for chunk in range(start, CHUNKS):
             cols_out(0, chunk)
 
-    def west_cols():
-        for chunk in range(CHUNKS):
-            cols_out(1, chunk)
-
     pl.when(wa == n_wa - 1)(send_rows)
     pl.when(jnp.logical_not(late | first_owner))(lambda: east_cols(0))
 
@@ -354,12 +351,6 @@
         east_cols(0)
 
     pl.when(wa == 1)(lambda: send_west(False))
-
-    for chunk in range(CHUNKS):
-        rim_grads(2, chunk)
-        corners_out(1, chunk)
-
-    west_cols()
 
     def gather_x():
         tfin[core, x] = zall[...]
@@ -367,8 +358,7 @@
             to = (x + step) % n_x
             remote(zall, tfin.at[core, x], xa_send.at[0], xa_recv.at[0], ha=2 * to + core).start()
 
-    @pl.when(is_owner)
-    def _():
+    def sum_z():
         zin[wa] = zpart[...]
         wait_bytes(zin.at[0:n_wa - 1], z_recv.at[0])
         final = zin[0]
@@ -383,14 +373,32 @@
         ((wa == 1) & (ha == 0), range(2, half + 2), n_x),
         ((wa == helper) & (ha == 0), range(half + 2, n_wa), 0),
     )
-    for cond, cols, rows in served[:3]:
-
-        @pl.when(cond)
-        def _():
-            for to in range(rows):
-                remote(zall, tfin.at[core, x], za_send.at[0], xa_recv.at[0], ha=2 * to, wa=0).start()
-            for col in cols:
-                remote(zall, zall, za_send.at[0], za_recv.at[0], wa=col).start()
+    def serve(which):
+        for cond, cols, rows in which:
+
+            @pl.when(cond)
+            def _():
+                for to in range(rows):
+                    remote(zall, tfin.at[core, x], za_send.at[0], xa_recv.at[0], ha=2 * to, wa=0).start()
+                for col in cols:
+                    remote(zall, zall, za_send.at[0], za_recv.at[0], wa=col).start()
+
+    for chunk in range(CHUNKS):
+        rim_grads(2, chunk)
+        corners_out(1, chunk)
+
+    @pl.when(first_owner)
+    def _():
+        sum_z()
+        serve(served[:1])
+
+    for chunk in range(CHUNKS):
+        cols_out(1, chunk)
+
+    @pl.when(wa == 1)
+    def _():
+        sum_z()
+        serve(served[1:3])
 
     @pl.when(wa >= 2)
     def _():

time: 77.6 us -> 75.7 us (0.976)
  Pallas kernels: 76.8 us -> 74.8 us
    pallas_call x1, Pallas kernels: 75.7 us -> 73.7 us  [local(): pl.pallas_call(functools.partial(kernel, n_ha, n_wa), out_shape=[vmem(fla...]
where the time goes in v4:
time: 75.7 us; the launch traced here: 75.5 us
  Pallas kernels  74.8 us (99%)
    pallas_call x1, Pallas kernels, local(): pl.pallas_call(functools.partial(kernel, n_ha, n_wa), out_shape=[vmem(fla...  73.7 us

profile of v4, /device:TPU:65, one launch (start us, length us, event | category | flops | bytes accessed | tf_op | source)
XLA Modules:
  0.0 75.5 jit_solution(3816870064140416524)
XLA Ops:
  0.6 73.7 %shard_map.146 = (bf16[128,1536]{1,0:T(8,128)(2,1)S(1)}, bf16[128,1536]{1,0:T(8,128)(2,1)S(1)}, bf16[128,1536]{1,0:T(8,128)(2,1)S(1)}, bf16[2,4,8,1536]{3,2,1,0:T(8,128)(2,1)S(1)}) custom-call(bf16[128,1536]{1,0:T(8,128)(2,1)} %bitcast.16, bf16[128,1536]{1,0:T(8,128)(2,1)} %bitcast.17, bf16[128,1536]{1,0:T(8,128)(2,1)} %bitcast.18, ...), custom_call_target="tpu_custom_call" | custom-call | tf_op jit(solution)/shard_map/pallas_call | solution.py:500
  74.4 1.1 %shard_map.147 = (bf16[128,1536]{1,0:T(8,128)(2,1)}, bf16[128,1536]{1,0:T(8,128)(2,1)}, bf16[128,1536]{1,0:T(8,128)(2,1)}, bf16[4,8,1536]{2,1,0:T(8,128)(2,1)}, bf16[4,8,1536]{2,1,0:T(8,128)(2,1)}) custom-call(bf16[128,1536]{1,0:T(8,128)(2,1)S(1)} %get-tuple-element.14.dq, bf16[128,1536]{1,0:T(8,128)(2,1)S(1)} %get-tuple-element.15.dk, ...), custom_call_target="tpu_custom_call" | custom-call | tf_op jit(solution)/shard_map/pallas_call | solution.py:531

commit v5 on v4

--- a/solution.py
+++ b/solution.py
@@ -83,6 +83,7 @@
     half, helper = n_wa // 2, n_wa // 4 + 1
     corner_device = (wa == 0) & (ha == 0)
     first_owner = (wa == 0) & (ha != 0)
+    meets = (wa == 0) | (wa == n_wa - 1)
     is_owner = first_owner | (wa == 1)
     greeters = jnp.where(ha == 0, 1, 2) - jnp.where(is_owner, 1, 0)
 
@@ -119,7 +120,7 @@
     signal(barrier, ha=up)
     signal(barrier, ha=down)
 
-    @pl.when(wa != 0)
+    @pl.when(jnp.logical_not(meets))
     def _():
         for step in range(1, n_x):
             signal(barrier, ha=(ha + 2 * step) % n_ha)
@@ -142,9 +143,9 @@
             ).start()
 
     def enter():
-        pl.semaphore_wait(barrier, 5 + greeters + jnp.where(wa == 0, 0, n_x - 1))
-
-        @pl.when(wa == 0)
+        pl.semaphore_wait(barrier, 5 + greeters + jnp.where(meets, 0, n_x - 1))
+
+        @pl.when(meets)
         def _():
             signal(met.at[0], ha=up)
             signal(met.at[0], ha=down)
@@ -241,7 +242,7 @@
     pl.when(jnp.logical_not(late))(send_rows)
     pl.when((wa >= 2) & (wa != n_wa - 1))(lambda: send_west(False))
 
-    @pl.when(wa == 0)
+    @pl.when(meets)
     def _():
         for at in range(len(distances) - 1):
             meet_row(at)

time: 75.7 us -> 74.6 us (0.985)
  Pallas kernels: 74.8 us -> 73.5 us
    pallas_call x1, Pallas kernels: 73.7 us -> 72.4 us  [local(): pl.pallas_call(functools.partial(kernel, n_ha, n_wa), out_shape=[vmem(fla...]
where the time goes in v5:
time: 74.6 us; the launch traced here: 74.1 us
  Pallas kernels  73.5 us (99%)
    pallas_call x1, Pallas kernels, local(): pl.pallas_call(functools.partial(kernel, n_ha, n_wa), out_shape=[vmem(fla...  72.4 us

profile of v5, /device:TPU:65, one launch (start us, length us, event | category | flops | bytes accessed | tf_op | source)
XLA Modules:
  0.0 74.1 jit_solution(10753815006953247355)
XLA Ops:
  0.6 72.4 %shard_map.146 = (bf16[128,1536]{1,0:T(8,128)(2,1)S(1)}, bf16[128,1536]{1,0:T(8,128)(2,1)S(1)}, bf16[128,1536]{1,0:T(8,128)(2,1)S(1)}, bf16[2,4,8,1536]{3,2,1,0:T(8,128)(2,1)S(1)}) custom-call(bf16[128,1536]{1,0:T(8,128)(2,1)} %bitcast.16, bf16[128,1536]{1,0:T(8,128)(2,1)} %bitcast.17, bf16[128,1536]{1,0:T(8,128)(2,1)} %bitcast.18, ...), custom_call_target="tpu_custom_call" | custom-call | tf_op jit(solution)/shard_map/pallas_call | solution.py:501
  73.0 1.1 %shard_map.147 = (bf16[128,1536]{1,0:T(8,128)(2,1)}, bf16[128,1536]{1,0:T(8,128)(2,1)}, bf16[128,1536]{1,0:T(8,128)(2,1)}, bf16[4,8,1536]{2,1,0:T(8,128)(2,1)}, bf16[4,8,1536]{2,1,0:T(8,128)(2,1)}) custom-call(bf16[128,1536]{1,0:T(8,128)(2,1)S(1)} %get-tuple-element.14.dq, bf16[128,1536]{1,0:T(8,128)(2,1)S(1)} %get-tuple-element.15.dk, ...), custom_call_target="tpu_custom_call" | custom-call | tf_op jit(solution)/shard_map/pallas_call | solution.py:532
